TPU v7x, 1024 devices: a whole 4x4x32 slice. The times are simulated.
1024 devices in a mesh: dp: 64 (over z, core), mp: 16 (over x, y).
Axes of the slice: x: 4, y: 4, z: 32, core: 2. Of those that a mesh axis runs over, the one named last changes fastest.
Arguments:
- block_input: bfloat16 [32768, 6144], P('dp', 'mp'), may hold values from -6 to 6
- prenorm_gain: float32 [6144], P('mp'), may hold values from 0.5 to 1.5
- weight: bfloat16 [6144, 3072], P('mp', 'dp'), may hold values from -0.078125 to 0.078125
- query: bfloat16 [32768, 3072], P('dp'), may hold values from -6 to 6
- grad_normed: bfloat16 [32768, 3072], P('dp'), may hold values from -6 to 6
- qk_gain: float32 [128], replicated, may hold values from 0.5 to 1.5
Outputs:
- input_gradient: bfloat16 [32768, 6144], P('dp', 'mp')
- grad_weight: float32 [6144, 3072], P('mp', 'dp')
- prenorm_gain_gradient: float32 [6144], P('mp')
- grad_qk_gain: float32 [128], replicated
All inputs are finite; a program needn't handle non-finite values.
Results may differ from a plain program's by a relative error of at most 0.0049.
Values may be sent and summed in bfloat16 or wider, within the bound.
No kernel may reach another device: no remote copies, remote signals or barrier semaphores. Data moves between devices by JAX's collectives and lax.ppermute only.
A program may use at most 64 MiB of HBM per device.

v0:
```python
import jax
import jax.numpy as jnp
from jax import lax
from jax.experimental import pallas as pl
from jax.experimental.pallas import tpu as pltpu
from jax.sharding import Mesh
from jax.sharding import PartitionSpec as P


D = 6144
EPS = 1e-06
HEAD = 128
FAR, NEAR = 8, 4
COLS = 48
MP = ("x", "y")
DP = ("far", "near", "core")


def qk_kernel(
    core_ref, query_ref, grad_ref, gain_ref, own_ref, other_ref, gain_grad_ref, rows_ref
):
    @pl.when(pl.program_id(0) == 0)
    def _():
        gain_grad_ref[...] = jnp.zeros_like(gain_grad_ref)

    core = core_ref[0]
    gain = gain_ref[...]
    scale = 1.0 / HEAD

    def three_heads(group, total):
        for j in range(3):
            cols = pl.ds(pl.multiple_of(group * 384 + j * HEAD, HEAD), HEAD)
            q = query_ref[:, cols].astype(jnp.float32)
            upstream = grad_ref[:, cols].astype(jnp.float32)
            mean = jnp.sum(q, axis=1, keepdims=True) * scale
            var = jnp.sum(q * q, axis=1, keepdims=True) * scale - mean * mean
            inv = lax.rsqrt(var + EPS)
            qhat = (q - mean) * inv
            dqhat = upstream * gain
            mean_d = jnp.sum(dqhat, axis=1, keepdims=True) * scale
            mean_c = jnp.sum(dqhat * qhat, axis=1, keepdims=True) * scale
            rows_ref[:, j * HEAD : (j + 1) * HEAD] = (
                inv * (dqhat - mean_d - qhat * mean_c)
            ).astype(jnp.bfloat16)
            total = total + jnp.sum((upstream * qhat).reshape(-1, 8, HEAD), axis=0)
        turned = jnp.transpose(rows_ref[...])
        for parity, (even_ref, odd_ref) in enumerate(((own_ref, other_ref), (other_ref, own_ref))):

            @pl.when(core == parity)
            def _():
                for b in range(8):
                    to_ref = odd_ref if b % 2 else even_ref
                    to_ref[b // 2, group] = turned[COLS * b : COLS * (b + 1)]

        return total

    zero = jnp.zeros((8, HEAD), jnp.float32)
    gain_grad_ref[...] += lax.fori_loop(0, FAR, three_heads, zero)


def qk_backward(core, query, grad_normed, qk_gain):
    tokens, width = query.shape
    block = 128
    return pl.pallas_call(
        qk_kernel,
        grid=(tokens // block,),
        in_specs=[
            pl.BlockSpec(memory_space=pltpu.SMEM),
            pl.BlockSpec((block, width), lambda i: (i, 0)),
            pl.BlockSpec((block, width), lambda i: (i, 0)),
            pl.BlockSpec((1, HEAD), lambda i: (0, 0)),
        ],
        out_specs=[
            pl.BlockSpec((NEAR, FAR, COLS, block), lambda i: (0, 0, 0, i)),
            pl.BlockSpec((NEAR, FAR, COLS, block), lambda i: (0, 0, 0, i)),
            pl.BlockSpec((8, HEAD), lambda i: (0, 0)),
        ],
        out_shape=[
            jax.ShapeDtypeStruct((NEAR, FAR, COLS, tokens), jnp.bfloat16),
            jax.ShapeDtypeStruct((NEAR, FAR, COLS, tokens), jnp.bfloat16),
            jax.ShapeDtypeStruct((8, HEAD), jnp.float32),
        ],
        scratch_shapes=[pltpu.VMEM((block, 3 * HEAD), jnp.bfloat16)],
        compiler_params=pltpu.CompilerParams(dimension_semantics=("arbitrary",)),
        cost_estimate=pl.CostEstimate(
            flops=60_000_000, bytes_accessed=9_500_000, transcendentals=12288
        ),
    )(core, query, grad_normed, qk_gain.reshape(1, HEAD))


def input_kernel(
    near_ref, own_ref, other_ref, query_own_ref, query_other_ref, x_ref, stat_ref, gain_ref,
    slope_ref, sums_ref, gains_ref, grad_ref,
):
    step = pl.program_id(0)

    def product(w_ref, q_ref):
        return lax.dot_general(
            w_ref[...], q_ref[0], (((0,), (0,)), ((), ())), preferred_element_type=jnp.float32
        )

    part = product(own_ref, query_own_ref) + product(other_ref, query_other_ref)

    @pl.when(step == 0)
    def _():
        grad_ref[...] = part

    @pl.when(step > 0)
    def _():
        grad_ref[...] += part

    @pl.when(step == NEAR - 1)
    def _():
        grad = grad_ref[...]
        xhat = (x_ref[...].astype(jnp.float32) - stat_ref[0:1]) * stat_ref[1:2]
        slope = grad * gain_ref[...]
        slope_ref[...] = slope
        sums_ref[0:1] = jnp.sum(slope, axis=0, keepdims=True)
        sums_ref[1:2] = jnp.sum(slope * xhat, axis=0, keepdims=True)
        cross = grad * xhat
        lanes = cross[:, :128] + cross[:, 128:256] + cross[:, 256:384] + cross[:, 384:]
        gains_ref[...] = jnp.sum(jnp.transpose(lanes), axis=0, keepdims=True)


def input_backward(near, own, other, query_own, query_other, x, stat, gain):
    rows, tokens = x.shape
    span = own.shape[0] // NEAR
    whole = lambda i, near: (0, 0)
    return pl.pallas_call(
        input_kernel,
        grid_spec=pltpu.PrefetchScalarGridSpec(
            num_scalar_prefetch=1,
            grid=(NEAR,),
            in_specs=[
                pl.BlockSpec((span, rows), lambda i, near: (i, 0)),
                pl.BlockSpec((span, rows), lambda i, near: (i, 0)),
                pl.BlockSpec((1, span, tokens), lambda i, near: ((near[0] + i) % NEAR, 0, 0)),
                pl.BlockSpec((1, span, tokens), lambda i, near: ((near[0] + i) % NEAR, 0, 0)),
                pl.BlockSpec((rows, tokens), whole),
                pl.BlockSpec((2, tokens), whole),
                pl.BlockSpec((rows, 1), whole),
            ],
            out_specs=[
                pl.BlockSpec((rows, tokens), whole),
                pl.BlockSpec((2, tokens), whole),
                pl.BlockSpec((1, rows), whole),
            ],
            scratch_shapes=[pltpu.VMEM((rows, tokens), jnp.float32)],
        ),
        out_shape=[
            jax.ShapeDtypeStruct((rows, tokens), jnp.float32),
            jax.ShapeDtypeStruct((2, tokens), jnp.float32),
            jax.ShapeDtypeStruct((1, rows), jnp.float32),
        ],
        compiler_params=pltpu.CompilerParams(dimension_semantics=("arbitrary",)),
        cost_estimate=pl.CostEstimate(
            flops=2_400_000_000, bytes_accessed=7_000_000, transcendentals=0
        ),
    )(near, own, other, query_own, query_other, x, stat, gain)


def exchange(x, axes):
    return lax.all_to_all(x, axes, 0, 0, tiled=True)


def shared_by(x, axes):
    copies = jnp.broadcast_to(x[None], (lax.axis_size(axes), *x.shape))
    return exchange(copies, axes)


def summed(x, axes):
    for axis in axes:
        x = jnp.sum(lax.all_gather(x, axis, axis=0), axis=0)
    return x


def swapped(x):
    return lax.ppermute(x, "core", [(0, 1), (1, 0)])


def from_chip(x, distance):
    chips = FAR * NEAR
    return lax.ppermute(x, ("far", "near"), [((i + distance) % chips, i) for i in range(chips)])


def shards(block_input, prenorm_gain, weight, query, grad_normed, qk_gain):
    tokens, rows = block_input.shape
    core = lax.axis_index("core").astype(jnp.int32).reshape(1)
    near = lax.axis_index("near").astype(jnp.int32).reshape(1)

    own = shared_by(weight.T, "far")
    after = from_chip(own, 1)
    before = from_chip(own, -1)
    half = FAR // 2
    across = [from_chip(own[:half], 2), from_chip(own[half:], -2)]
    own = jnp.concatenate([own, after, *across, before]).reshape(-1, rows)
    other = swapped(own)

    x_turned = block_input.T
    x = x_turned.astype(jnp.float32)
    sums = jnp.concatenate([jnp.sum(x, axis=0), jnp.sum(x * x, axis=0)]).reshape(8, 128)
    sums = summed(sums, MP)
    sums = sums.reshape(2, tokens)

    query_own, query_other, qk_partial = qk_backward(core, query, grad_normed, qk_gain)

    mean = sums[0:1] / D
    inv = lax.rsqrt(sums[1:2] / D - mean * mean + EPS)
    xhat = (x - mean) * inv
    gain = prenorm_gain[:, None]
    normed = (xhat * gain).astype(jnp.bfloat16)

    def weight_part(grad_query):
        return lax.dot_general(
            grad_query.reshape(-1, tokens), normed, (((1,), (1,)), ((), ())),
            preferred_element_type=jnp.float32,
        )

    part = weight_part(query_other).astype(jnp.bfloat16)
    from_core = swapped(part)
    part = weight_part(query_own) + from_core.astype(jnp.float32)
    part = part.astype(jnp.bfloat16).reshape(NEAR, FAR, COLS, rows)
    part = exchange(part, "near")
    part = jnp.sum(part.astype(jnp.float32), axis=0).astype(jnp.bfloat16)
    part = exchange(part, "far")
    grad_weight = jnp.sum(part.astype(jnp.float32), axis=0).T

    slope, slopes, gains = input_backward(
        near, own, other, query_own.reshape(NEAR, -1, tokens),
        query_other.reshape(NEAR, -1, tokens), x_turned, jnp.concatenate([mean, inv]), gain,
    )
    slopes = summed(slopes.reshape(8, 128), MP).reshape(2, tokens) / D
    input_gradient = (inv * (slope - slopes[0:1] - xhat * slopes[1:2])).astype(jnp.bfloat16).T

    gains = jnp.concatenate([gains[0], jnp.sum(qk_partial, axis=0)]).reshape(4, 128)
    gains = summed(gains + swapped(gains), ("near", "far")).reshape(-1)
    return (input_gradient, grad_weight, gains[:rows], gains[rows:])


def solution(mesh):
    finer = Mesh(mesh.devices.reshape(FAR, NEAR, 2, 4, 4), (*DP, *MP))
    in_specs = (P(DP, MP), P(MP), P(MP, DP), P(DP, None), P(DP, None), P())
    out_specs = (P(DP, MP), P(MP, DP), P(MP), P())

    return jax.shard_map(
        shards, mesh=finer, in_specs=in_specs, out_specs=out_specs, check_vma=False
    )
```

profile of v0, /device:TPU:8, one launch (start us, length us, event | category | flops | bytes accessed | tf_op | source)
XLA Modules:
  0.0 247.0 jit_solution(2505737719265773605)
XLA Ops:
  0.6 1.6 broadcast_in_dim.4
  2.2 28.3 %all-to-all-start = ((bf16[8,48,384]{2,1,0:T(8,128)(2,1)}), bf16[8,48,384]{2,1,0:T(8,128)(2,1)S(1)}, u32[]{:S(2)}, u32[]{:S(2)}) async-start(bf16[8,48,384]{2,1,0:T(8,128)(2,1)} %broadcast_in_dim.4), calls=%async_computation | async-start | bytes 589824 | tf_op jit(solution)/shard_map/all_to_all | solution.py:163
  30.9 12.4 %all_gather.30 = f32[4,8,128]{2,1,0:T(8,128)S(1)} all-gather(f32[1,8,128]{2,1,0:T(8,128)S(1)} %maximum_bitcast_fusion), channel_id=1, replica_groups=mesh['far'=8,'near'=4,'core'=2,'x'=4,'y'=4] {'x'}, dimensions={0}, use_global_device_ids=true | all-gather | bytes 20480 | tf_op jit(solution)/shard_map/all_gather | solution.py:173
  43.3 12.2 %all-gather = f32[32,128]{1,0:T(8,128)S(1)} all-gather(f32[8,128]{1,0:T(8,128)S(1)} %reduce_sum.104), channel_id=2, replica_groups=mesh['far'=8,'near'=4,'core'=2,'x'=4,'y'=4] {'y'}, dimensions={0}, use_global_device_ids=true | all-gather | bytes 20480 | tf_op jit(solution)/shard_map/all_gather | solution.py:173
  55.5 16.5 %shard_map.93 = (bf16[4,8,48,512]{3,2,1,0:T(8,128)(2,1)}, bf16[4,8,48,512]{3,2,1,0:T(8,128)(2,1)}, f32[8,128]{1,0:T(8,128)}) custom-call(s32[1]{0:T(128)} %bitcast.8.core_ref, bf16[512,3072]{1,0:T(8,128)(2,1)} %query_ref.1, bf16[512,3072]{1,0:T(8,128)(2,1)} %grad_ref.1, f32[1,128]{1,0:T(1,128)} %bitcast.68), custom_call_target="tpu_custom_call" | custom-call | flops 60000000 | bytes 9500000 | tf_op jit(solution)/shard_map/pallas_call | solution.py:64
  72.0 2.6 %convolution_convert_fusion = bf16[1536,384]{1,0:T(8,128)(2,1)S(1)} fusion(bf16[1536,512]{1,0:T(8,128)(2,1)} %bitcast.71, f32[384]{0:T(512)S(1)} %copy-done.5, f32[512]{0:T(512)S(1)} %get-tuple-element.38, f32[512]{0:T(512)S(1)} %fusion.15, bf16[512,384]{0,1:T(8,128)(2,1)S(1)} %copy.18), kind=kOutput, calls=%fused_computation | convolution fusion | flops 605552640 | bytes 3151360 | tf_op jit(solution)/shard_map/dot_general | solution.py:214
  74.6 1.9 collective-permute-start.5
  76.6 2.8 %collective-permute-done.5 = bf16[1536,384]{1,0:T(8,128)(2,1)S(1)} collective-permute-done((bf16[1536,384]{1,0:T(8,128)(2,1)S(1)}, bf16[1536,384]{1,0:T(8,128)(2,1)S(1)}, u32[]{:S(2)}, u32[]{:S(2)}) %collective-permute-start.5) | collective-permute-done | bytes 1179680 | tf_op jit(solution)/shard_map/ppermute | solution.py:178
  79.4 2.2 add_convert_fusion
  81.5 3.5 %all-to-all-start.1 = ((bf16[4,8,48,384]{3,2,1,0:T(8,128)(2,1)}), bf16[4,8,48,384]{3,2,1,0:T(8,128)(2,1)S(1)}, u32[]{:S(2)}, u32[]{:S(2)}) async-start(bf16[4,8,48,384]{3,2,1,0:T(8,128)(2,1)} %bitcast.20), calls=%async_computation.1 | async-start | bytes 2359296 | tf_op jit(solution)/shard_map/all_to_all | solution.py:163
  85.1 8.4 %collective-permute-start = (bf16[8,48,384]{2,1,0:T(8,128)(2,1)S(1)}, bf16[8,48,384]{2,1,0:T(8,128)(2,1)S(1)}, u32[]{:S(2)}, u32[]{:S(2)}) collective-permute-start(bf16[8,48,384]{2,1,0:T(8,128)(2,1)S(1)} %all-to-all-done), channel_id=1, source_target_pairs={{32,0},{64,32},{96,64},{128,96},{160,128},{192,160},{224,192},{256... | collective-permute-start | bytes 884744 | tf_op jit(solution)/shard_map/ppermute | solution.py:183
  93.5 1.9 collective-permute-start.2
  95.4 6.0 %collective-permute-start.1 = (bf16[4,48,384]{2,1,0:T(8,128)(2,1)S(1)}, bf16[4,48,384]{2,1,0:T(8,128)(2,1)S(1)}, u32[]{:S(2)}, u32[]{:S(2)}) collective-permute-start(bf16[4,48,384]{2,1,0:T(8,128)(2,1)S(1)} %get-tuple-element.35), channel_id=1, source_target_pairs={{64,0},{96,32},{128,64},{160,96},{192,128},{224,160},{256,192},{28... | collective-permute-start | bytes 442376 | tf_op jit(solution)/shard_map/ppermute | solution.py:183
  101.5 1.9 collective-permute-start.3
  103.4 9.2 %collective-permute-done = bf16[8,48,384]{2,1,0:T(8,128)(2,1)S(1)} collective-permute-done((bf16[8,48,384]{2,1,0:T(8,128)(2,1)S(1)}, bf16[8,48,384]{2,1,0:T(8,128)(2,1)S(1)}, u32[]{:S(2)}, u32[]{:S(2)}) %collective-permute-start) | collective-permute-done | bytes 294944 | tf_op jit(solution)/shard_map/ppermute | solution.py:183
  112.6 14.2 %collective-permute-done.1 = bf16[4,48,384]{2,1,0:T(8,128)(2,1)S(1)} collective-permute-done((bf16[4,48,384]{2,1,0:T(8,128)(2,1)S(1)}, bf16[4,48,384]{2,1,0:T(8,128)(2,1)S(1)}, u32[]{:S(2)}, u32[]{:S(2)}) %collective-permute-start.1) | collective-permute-done | bytes 147488 | tf_op jit(solution)/shard_map/ppermute | solution.py:183
  127.0 2.1 collective-permute-start.4
  130.0 21.6 %all-to-all-start.2 = ((bf16[8,48,384]{2,1,0:T(8,128)(2,1)}), bf16[8,48,384]{2,1,0:T(8,128)(2,1)S(1)}, u32[]{:S(2)}, u32[]{:S(2)}) async-start(bf16[8,48,384]{2,1,0:T(8,128)(2,1)} %reduce_sum.108), calls=%async_computation.2 | async-start | bytes 589824 | tf_op jit(solution)/shard_map/all_to_all | solution.py:163
  153.1 6.4 %shard_map.94 = (f32[384,512]{1,0:T(8,128)}, f32[2,512]{1,0:T(2,128)}, f32[1,384]{1,0:T(1,128)}) custom-call(s32[1]{0:T(128)} %bitcast.5.near_ref, bf16[1536,384]{1,0:T(8,128)(2,1)} %bitcast.61, bf16[1536,384]{1,0:T(8,128)(2,1)} %collective-permute-done.4.other_ref, bf16[4,384,512]{2,1,0:T(8,128)(2,1)} %bitcast.69, bf16[4,384,512]{2,1,0:T(8,128)(2,1)} %bitcast.72, ...), custom_call_target="tpu_custom_call" | custom-call | flops 2400000000 | bytes 7000000 | tf_op jit(solution)/shard_map/pallas_call | solution.py:129
  160.9 2.1 collective-permute-start.6
  163.0 12.0 %all_gather.33 = f32[4,8,128]{2,1,0:T(8,128)S(1)} all-gather(f32[1,8,128]{2,1,0:T(8,128)S(1)} %all_gather_reshape.7), channel_id=1, replica_groups=mesh['far'=8,'near'=4,'core'=2,'x'=4,'y'=4] {'x'}, dimensions={0}, use_global_device_ids=true | all-gather | bytes 20480 | tf_op jit(solution)/shard_map/all_gather | solution.py:173
  175.0 12.0 %all-gather.1 = f32[32,128]{1,0:T(8,128)S(1)} all-gather(f32[8,128]{1,0:T(8,128)S(1)} %reduce_sum.106), channel_id=3, replica_groups=mesh['far'=8,'near'=4,'core'=2,'x'=4,'y'=4] {'y'}, dimensions={0}, use_global_device_ids=true | all-gather | bytes 20480 | tf_op jit(solution)/shard_map/all_gather | solution.py:173
  189.3 11.9 %all-gather.4 = f32[4,4,128]{2,1,0:T(4,128)S(1)} all-gather(f32[1,4,128]{2,1,0:T(4,128)S(1)} %add_bitcast_fusion), channel_id=4, replica_groups=mesh['far'=8,'near'=4,'core'=2,'x'=4,'y'=4] {'near'}, dimensions={0}, use_global_device_ids=true | all-gather | bytes 10240 | tf_op jit(solution)/shard_map/all_gather | solution.py:173
  201.3 43.9 %all-gather.5 = f32[8,4,128]{2,1,0:T(4,128)S(1)} all-gather(f32[1,4,128]{2,1,0:T(4,128)S(1)} %bitcast.67), channel_id=5, replica_groups=mesh['far'=8,'near'=4,'core'=2,'x'=4,'y'=4] {'far'}, dimensions={0}, use_global_device_ids=true | all-gather | bytes 18432 | tf_op jit(solution)/shard_map/all_gather | solution.py:173
  (54 shorter events, 8.5 us)
Async XLA Ops:
  0.6 29.9 %copy-start.2 = (bf16[512,384]{1,0:T(8,128)(2,1)S(1)}, bf16[512,384]{1,0:T(8,128)(2,1)}, u32[]{:S(2)}) copy-start(bf16[512,384]{1,0:T(8,128)(2,1)} %param.6) | copy-start | bytes 1179652
  2.2 79.3 %all-to-all-start = ((bf16[8,48,384]{2,1,0:T(8,128)(2,1)}), bf16[8,48,384]{2,1,0:T(8,128)(2,1)S(1)}, u32[]{:S(2)}, u32[]{:S(2)}) async-start(bf16[8,48,384]{2,1,0:T(8,128)(2,1)} %broadcast_in_dim.4), calls=%async_computation | async-start | bytes 589824 | tf_op jit(solution)/shard_map/all_to_all | solution.py:163
  30.8 48.6 %copy-start = (bf16[512,384]{0,1:T(8,128)(2,1)}, bf16[512,384]{0,1:T(8,128)(2,1)S(1)}, u32[]{:S(2)}) copy-start(bf16[512,384]{0,1:T(8,128)(2,1)S(1)} %copy.18) | copy-start | bytes 1179652
  55.5 16.5 %copy-start.5 = (f32[384]{0:T(512)S(1)}, f32[384]{0:T(512)}, u32[]{:S(2)}) copy-start(f32[384]{0:T(512)} %param.7) | copy-start | bytes 4612
  72.0 7.4 %copy-start.6 = (bf16[4,8,48,512]{3,2,1,0:T(8,128)(2,1)S(1)}, bf16[4,8,48,512]{3,2,1,0:T(8,128)(2,1)}, u32[]{:S(2)}) copy-start(bf16[4,8,48,512]{3,2,1,0:T(8,128)(2,1)} %get-tuple-element.10) | copy-start | bytes 4718596
  74.6 4.7 %collective-permute-start.5 = (bf16[1536,384]{1,0:T(8,128)(2,1)S(1)}, bf16[1536,384]{1,0:T(8,128)(2,1)S(1)}, u32[]{:S(2)}, u32[]{:S(2)}) collective-permute-start(bf16[1536,384]{1,0:T(8,128)(2,1)S(1)} %convolution_convert_fusion), channel_id=1, source_target_pairs={{0,16},{16,0},{1,17},{17,1},{2,18},{18,2},{3,19},{19,3},{4,20},{20... | collective-permute-start | bytes 3538952 | tf_op jit(solution)/shard_map/ppermute | solution.py:178
  81.5 47.5 %all-to-all-start.1 = ((bf16[4,8,48,384]{3,2,1,0:T(8,128)(2,1)}), bf16[4,8,48,384]{3,2,1,0:T(8,128)(2,1)S(1)}, u32[]{:S(2)}, u32[]{:S(2)}) async-start(bf16[4,8,48,384]{3,2,1,0:T(8,128)(2,1)} %bitcast.20), calls=%async_computation.1 | async-start | bytes 2359296 | tf_op jit(solution)/shard_map/all_to_all | solution.py:163
  85.1 27.5 %collective-permute-start = (bf16[8,48,384]{2,1,0:T(8,128)(2,1)S(1)}, bf16[8,48,384]{2,1,0:T(8,128)(2,1)S(1)}, u32[]{:S(2)}, u32[]{:S(2)}) collective-permute-start(bf16[8,48,384]{2,1,0:T(8,128)(2,1)S(1)} %all-to-all-done), channel_id=1, source_target_pairs={{32,0},{64,32},{96,64},{128,96},{160,128},{192,160},{224,192},{256... | collective-permute-start | bytes 884744 | tf_op jit(solution)/shard_map/ppermute | solution.py:183
  93.5 33.4 %collective-permute-start.2 = (bf16[4,48,384]{2,1,0:T(8,128)(2,1)S(1)}, bf16[4,48,384]{2,1,0:T(8,128)(2,1)S(1)}, u32[]{:S(2)}, u32[]{:S(2)}) collective-permute-start(bf16[4,48,384]{2,1,0:T(8,128)(2,1)S(1)} %get-tuple-element.34), channel_id=1, source_target_pairs={{960,0},{992,32},{0,64},{32,96},{64,128},{96,160},{128,192},{160,2... | collective-permute-start | bytes 442376 | tf_op jit(solution)/shard_map/ppermute | solution.py:183
  95.4 31.4 %collective-permute-start.1 = (bf16[4,48,384]{2,1,0:T(8,128)(2,1)S(1)}, bf16[4,48,384]{2,1,0:T(8,128)(2,1)S(1)}, u32[]{:S(2)}, u32[]{:S(2)}) collective-permute-start(bf16[4,48,384]{2,1,0:T(8,128)(2,1)S(1)} %get-tuple-element.35), channel_id=1, source_target_pairs={{64,0},{96,32},{128,64},{160,96},{192,128},{224,160},{256,192},{28... | collective-permute-start | bytes 442376 | tf_op jit(solution)/shard_map/ppermute | solution.py:183
  101.5 25.5 %collective-permute-start.3 = (bf16[8,48,384]{2,1,0:T(8,128)(2,1)S(1)}, bf16[8,48,384]{2,1,0:T(8,128)(2,1)S(1)}, u32[]{:S(2)}, u32[]{:S(2)}) collective-permute-start(bf16[8,48,384]{2,1,0:T(8,128)(2,1)S(1)} %all-to-all-done), channel_id=1, source_target_pairs={{992,0},{0,32},{32,64},{64,96},{96,128},{128,160},{160,192},{192,2... | collective-permute-start | bytes 884744 | tf_op jit(solution)/shard_map/ppermute | solution.py:183
  127.0 26.1 %copy-start.3 = (bf16[32,48,384]{2,1,0:T(8,128)(2,1)}, bf16[32,48,384]{2,1,0:T(8,128)(2,1)S(1)}, u32[]{:S(2)}) copy-start(bf16[32,48,384]{2,1,0:T(8,128)(2,1)S(1)} %constant_dynamic-update-slice_fusion) | copy-start | bytes 3538948
  127.0 25.5 %copy-start.4 = (f32[8,128]{1,0:T(8,128)S(1)}, f32[8,128]{1,0:T(8,128)}, u32[]{:S(2)}) copy-start(f32[8,128]{1,0:T(8,128)} %get-tuple-element.15) | copy-start | bytes 12292
  127.0 26.1 %collective-permute-start.4 = (bf16[1536,384]{1,0:T(8,128)(2,1)S(1)}, bf16[1536,384]{1,0:T(8,128)(2,1)}, u32[]{:S(2)}, u32[]{:S(2)}) collective-permute-start(bf16[1536,384]{1,0:T(8,128)(2,1)S(1)} %bitcast.60), channel_id=1, source_target_pairs={{0,16},{16,0},{1,17},{17,1},{2,18},{18,2},{3,19},{19,3},{4,20},{20... | collective-permute-start | bytes 3538952 | tf_op jit(solution)/shard_map/ppermute | solution.py:178
  130.0 116.3 %all-to-all-start.2 = ((bf16[8,48,384]{2,1,0:T(8,128)(2,1)}), bf16[8,48,384]{2,1,0:T(8,128)(2,1)S(1)}, u32[]{:S(2)}, u32[]{:S(2)}) async-start(bf16[8,48,384]{2,1,0:T(8,128)(2,1)} %reduce_sum.108), calls=%async_computation.2 | async-start | bytes 589824 | tf_op jit(solution)/shard_map/all_to_all | solution.py:163
  153.1 34.0 %copy-start.1 = (bf16[512,384]{0,1:T(8,128)(2,1)S(1)}, bf16[512,384]{0,1:T(8,128)(2,1)}, u32[]{:S(2)}) copy-start(bf16[512,384]{0,1:T(8,128)(2,1)} %copy-done) | copy-start | bytes 1179652
  160.9 28.5 %collective-permute-start.6 = (f32[4,128]{1,0:T(4,128)S(1)}, f32[4,128]{1,0:T(4,128)S(1)}, u32[]{:S(2)}, u32[]{:S(2)}) collective-permute-start(f32[4,128]{1,0:T(4,128)S(1)} %maximum_bitcast_fusion.1), channel_id=1, source_target_pairs={{0,16},{16,0},{1,17},{17,1},{2,18},{18,2},{3,19},{19,3},{4,20},{20... | collective-permute-start | bytes 6152 | tf_op jit(solution)/shard_map/ppermute | solution.py:178
where the time goes:
time: 248 us; the launch traced here: 247 us
  blocking collectives  104 us (42%)
  starting transfers between devices  77.8 us (31%)
  waiting for transfers between devices  26.2 us (11%)
  Pallas kernels  22.8 us (9%)
  local copies, waits for them, and re-layouts  5.51 us (2%)
  matrix products  4.76 us (2%)
  other arithmetic  4.54 us (2%)
    all_gather x6, blocking collectives, summed(): x = jnp.sum(lax.all_gather(x, axis, axis=0), axis=0)  104 us
    all_to_all x3, starting transfers between devices, exchange(): return lax.all_to_all(x, axes, 0, 0, tiled=True)  53.5 us
    ppermute x4, waiting for transfers between devices, from_chip(): lax.ppermute(x, ('far', 'near'), [((i + distance) % chips, i) for i in ra...  23.4 us
    ppermute x4, starting transfers between devices, from_chip(): lax.ppermute(x, ('far', 'near'), [((i + distance) % chips, i) for i in ra...  18.2 us
    pallas_call x1, Pallas kernels, qk_backward(): pl.pallas_call(qk_kernel, grid=(tokens // block,), in_specs=[pl.BlockSpec...  16.5 us
    pallas_call x1, Pallas kernels, input_backward(): pl.pallas_call(input_kernel, grid_spec=pltpu.PrefetchScalarGridSpec(num_s...  6.38 us
    ppermute x3, starting transfers between devices, swapped(): return lax.ppermute(x, 'core', [(0, 1), (1, 0)])  6.1 us
  transfers between devices with their start and end apart: 10, of which 3 were waited for; matrix products, arithmetic and copies ran while one was open for 5% of the time, Pallas kernels for 9%

commit v1 on v0

--- a/solution.py
+++ b/solution.py
@@ -13,7 +13,7 @@
 FAR, NEAR = 8, 4
 COLS = 48
 MP = ("x", "y")
-DP = ("far", "near", "core")
+DP = ("far", "high", "low", "core")
 
 
 def qk_kernel(
@@ -88,30 +88,43 @@
     )(core, query, grad_normed, qk_gain.reshape(1, HEAD))
 
 
+def set_product(core, query_own_ref, query_other_ref):
+    def product(w_ref, owner, q_ref):
+        w = w_ref[:, owner].reshape(-1, w_ref.shape[-1])
+        q = q_ref[0].reshape(-1, q_ref.shape[-1])
+        return lax.dot_general(w, q, (((0,), (0,)), ((), ())), preferred_element_type=jnp.float32)
+
+    def both(w_ref):
+        return product(w_ref, core, query_own_ref) + product(w_ref, 1 - core, query_other_ref)
+
+    return both
+
+
+def first_kernel(at_ref, even_ref, odd_ref, query_own_ref, query_other_ref, out_ref):
+    both = set_product(at_ref[0], query_own_ref, query_other_ref)
+
+    @pl.when(pl.program_id(0) == 0)
+    def _():
+        out_ref[...] = both(even_ref)
+
+    @pl.when(pl.program_id(0) == 1)
+    def _():
+        out_ref[...] += both(odd_ref)
+
+
 def input_kernel(
-    near_ref, own_ref, other_ref, query_own_ref, query_other_ref, x_ref, stat_ref, gain_ref,
+    at_ref, even_ref, odd_ref, query_own_ref, query_other_ref, first_ref, x_ref, stat_ref, gain_ref,
     slope_ref, sums_ref, gains_ref, grad_ref,
 ):
-    step = pl.program_id(0)
-
-    def product(w_ref, q_ref):
-        return lax.dot_general(
-            w_ref[...], q_ref[0], (((0,), (0,)), ((), ())), preferred_element_type=jnp.float32
-        )
-
-    part = product(own_ref, query_own_ref) + product(other_ref, query_other_ref)
-
-    @pl.when(step == 0)
-    def _():
-        grad_ref[...] = part
-
-    @pl.when(step > 0)
-    def _():
-        grad_ref[...] += part
-
-    @pl.when(step == NEAR - 1)
-    def _():
-        grad = grad_ref[...]
+    both = set_product(at_ref[0], query_own_ref, query_other_ref)
+
+    @pl.when(pl.program_id(0) == 0)
+    def _():
+        grad_ref[...] = first_ref[...] + both(even_ref)
+
+    @pl.when(pl.program_id(0) == 1)
+    def _():
+        grad = grad_ref[...] + both(odd_ref)
         xhat = (x_ref[...].astype(jnp.float32) - stat_ref[0:1]) * stat_ref[1:2]
         slope = grad * gain_ref[...]
         slope_ref[...] = slope
@@ -122,41 +135,30 @@
         gains_ref[...] = jnp.sum(jnp.transpose(lanes), axis=0, keepdims=True)
 
 
-def input_backward(near, own, other, query_own, query_other, x, stat, gain):
-    rows, tokens = x.shape
-    span = own.shape[0] // NEAR
-    whole = lambda i, near: (0, 0)
+def input_part(body, at, even, odd, query_own, query_other, extra, outs, scratch):
+    tokens = query_own.shape[-1]
+    span = query_own.shape[1:]
+
+    def whole(shape):
+        return pl.BlockSpec(shape, lambda i, at: (0,) * len(shape))
+
+    query_spec = pl.BlockSpec((1, *span), lambda i, at: (2 * i + at[1], 0, 0, 0))
     return pl.pallas_call(
-        input_kernel,
+        body,
         grid_spec=pltpu.PrefetchScalarGridSpec(
             num_scalar_prefetch=1,
-            grid=(NEAR,),
-            in_specs=[
-                pl.BlockSpec((span, rows), lambda i, near: (i, 0)),
-                pl.BlockSpec((span, rows), lambda i, near: (i, 0)),
-                pl.BlockSpec((1, span, tokens), lambda i, near: ((near[0] + i) % NEAR, 0, 0)),
-                pl.BlockSpec((1, span, tokens), lambda i, near: ((near[0] + i) % NEAR, 0, 0)),
-                pl.BlockSpec((rows, tokens), whole),
-                pl.BlockSpec((2, tokens), whole),
-                pl.BlockSpec((rows, 1), whole),
-            ],
-            out_specs=[
-                pl.BlockSpec((rows, tokens), whole),
-                pl.BlockSpec((2, tokens), whole),
-                pl.BlockSpec((1, rows), whole),
-            ],
-            scratch_shapes=[pltpu.VMEM((rows, tokens), jnp.float32)],
+            grid=(2,),
+            in_specs=[whole(even.shape), whole(odd.shape), query_spec, query_spec]
+            + [whole(e.shape) for e in extra],
+            out_specs=[whole(o) for o in outs],
+            scratch_shapes=scratch,
         ),
-        out_shape=[
-            jax.ShapeDtypeStruct((rows, tokens), jnp.float32),
-            jax.ShapeDtypeStruct((2, tokens), jnp.float32),
-            jax.ShapeDtypeStruct((1, rows), jnp.float32),
-        ],
+        out_shape=[jax.ShapeDtypeStruct(o, jnp.float32) for o in outs],
         compiler_params=pltpu.CompilerParams(dimension_semantics=("arbitrary",)),
         cost_estimate=pl.CostEstimate(
-            flops=2_400_000_000, bytes_accessed=7_000_000, transcendentals=0
+            flops=2 * 1536 * 384 * tokens, bytes_accessed=4_500_000, transcendentals=0
         ),
-    )(near, own, other, query_own, query_other, x, stat, gain)
+    )(at, even, odd, query_own, query_other, *extra)
 
 
 def exchange(x, axes):
@@ -180,29 +182,27 @@
 
 def from_chip(x, distance):
     chips = FAR * NEAR
-    return lax.ppermute(x, ("far", "near"), [((i + distance) % chips, i) for i in range(chips)])
+    return lax.ppermute(x, ("far", "high", "low"), [((i + distance) % chips, i) for i in range(chips)])
 
 
 def shards(block_input, prenorm_gain, weight, query, grad_normed, qk_gain):
     tokens, rows = block_input.shape
-    core = lax.axis_index("core").astype(jnp.int32).reshape(1)
-    near = lax.axis_index("near").astype(jnp.int32).reshape(1)
-
-    own = shared_by(weight.T, "far")
-    after = from_chip(own, 1)
-    before = from_chip(own, -1)
-    half = FAR // 2
-    across = [from_chip(own[:half], 2), from_chip(own[half:], -2)]
-    own = jnp.concatenate([own, after, *across, before]).reshape(-1, rows)
-    other = swapped(own)
+    core = lax.axis_index("core").astype(jnp.int32)
+    parity = lax.axis_index("low").astype(jnp.int32)
+
+    mine = lax.all_gather(weight.T, ("far", "high", "core"), axis=0)
+    mine = mine.reshape(FAR, 2, 2, COLS, rows)
+    even, odd = mine[:, 0], mine[:, 1]
+    theirs_even = from_chip(even, 1)
+    theirs_odd = from_chip(odd, -1)
 
     x_turned = block_input.T
     x = x_turned.astype(jnp.float32)
     sums = jnp.concatenate([jnp.sum(x, axis=0), jnp.sum(x * x, axis=0)]).reshape(8, 128)
-    sums = summed(sums, MP)
-    sums = sums.reshape(2, tokens)
-
-    query_own, query_other, qk_partial = qk_backward(core, query, grad_normed, qk_gain)
+    sums = shared_by(sums, MP)
+    sums = jnp.sum(sums, axis=0).reshape(2, tokens)
+
+    query_own, query_other, qk_partial = qk_backward(core.reshape(1), query, grad_normed, qk_gain)
 
     mean = sums[0:1] / D
     inv = lax.rsqrt(sums[1:2] / D - mean * mean + EPS)
@@ -220,25 +220,32 @@
     from_core = swapped(part)
     part = weight_part(query_own) + from_core.astype(jnp.float32)
     part = part.astype(jnp.bfloat16).reshape(NEAR, FAR, COLS, rows)
-    part = exchange(part, "near")
+    part = exchange(part, ("high", "low"))
     part = jnp.sum(part.astype(jnp.float32), axis=0).astype(jnp.bfloat16)
     part = exchange(part, "far")
     grad_weight = jnp.sum(part.astype(jnp.float32), axis=0).T
 
-    slope, slopes, gains = input_backward(
-        near, own, other, query_own.reshape(NEAR, -1, tokens),
-        query_other.reshape(NEAR, -1, tokens), x_turned, jnp.concatenate([mean, inv]), gain,
+    (first,) = input_part(
+        first_kernel, jnp.stack([core, parity]), even, odd, query_own, query_other,
+        (), ((rows, tokens),), (),
+    )
+    slope, slopes, gains = input_part(
+        input_kernel, jnp.stack([core, 1 - parity]), theirs_even, theirs_odd,
+        query_own, query_other, (first, x_turned, jnp.concatenate([mean, inv]), gain),
+        ((rows, tokens), (2, tokens), (1, rows)), (pltpu.VMEM((rows, tokens), jnp.float32),),
     )
     slopes = summed(slopes.reshape(8, 128), MP).reshape(2, tokens) / D
     input_gradient = (inv * (slope - slopes[0:1] - xhat * slopes[1:2])).astype(jnp.bfloat16).T
 
     gains = jnp.concatenate([gains[0], jnp.sum(qk_partial, axis=0)]).reshape(4, 128)
-    gains = summed(gains + swapped(gains), ("near", "far")).reshape(-1)
+    gains = gains + swapped(gains)
+    gains = shared_by(gains, ("far", "high", "low"))
+    gains = jnp.sum(gains, axis=0).reshape(-1)
     return (input_gradient, grad_weight, gains[:rows], gains[rows:])
 
 
 def solution(mesh):
-    finer = Mesh(mesh.devices.reshape(FAR, NEAR, 2, 4, 4), (*DP, *MP))
+    finer = Mesh(mesh.devices.reshape(FAR, 2, 2, 2, 4, 4), (*DP, *MP))
     in_specs = (P(DP, MP), P(MP), P(MP, DP), P(DP, None), P(DP, None), P())
     out_specs = (P(DP, MP), P(MP, DP), P(MP), P())
 

time: 248 us -> 276 us (1.11)
  the two profiles are of different devices: /device:TPU:8 before, /device:TPU:32 now
where the time goes in v1:
time: 276 us
  waiting for transfers between devices  145 us (53%)
  starting transfers between devices  47.2 us (17%)
  Pallas kernels  25.9 us (9%)
  blocking collectives  24.6 us (9%)
  between operations  14.2 us (5%)
  local copies, waits for them, and re-layouts  8.2 us (3%)
  other arithmetic  5.32 us (2%)
  matrix products  4.76 us (2%)
    all_gather x1, waiting for transfers between devices, shards(): mine = lax.all_gather(weight.T, ('far', 'high', 'core'), axis=0)  95.4 us
    all_to_all x4, waiting for transfers between devices, exchange(): return lax.all_to_all(x, axes, 0, 0, tiled=True)  38.6 us
    all_to_all x4, starting transfers between devices, exchange(): return lax.all_to_all(x, axes, 0, 0, tiled=True)  37.4 us
    all_gather x2, blocking collectives, summed(): x = jnp.sum(lax.all_gather(x, axis, axis=0), axis=0)  24.6 us
    pallas_call x1, Pallas kernels, qk_backward(): pl.pallas_call(qk_kernel, grid=(tokens // block,), in_specs=[pl.BlockSpec...  16.5 us
    pallas_call x2, Pallas kernels, input_part(): pl.pallas_call(body, grid_spec=pltpu.PrefetchScalarGridSpec(num_scalar_pr...  9.38 us
    ppermute x2, waiting for transfers between devices, from_chip(): lax.ppermute(x, ('far', 'high', 'low'), [((i + distance) % chips, i) for...  6.82 us
    ppermute x2, starting transfers between devices, from_chip(): lax.ppermute(x, ('far', 'high', 'low'), [((i + distance) % chips, i) for...  5.97 us
  transfers between devices with their start and end apart: 9, of which 7 were waited for; matrix products, arithmetic and copies ran while one was open for 3% of the time, Pallas kernels for 9%

profile of v1, /device:TPU:32, one launch (start us, length us, event | category | flops | bytes accessed | tf_op | source)
XLA Modules:
  0.0 275.7 jit_solution(5144246054322802130)
XLA Ops:
  9.2 7.0 %all-to-all-start = ((f32[16,8,128]{2,1,0:T(8,128)}), f32[16,8,128]{2,1,0:T(8,128)S(1)}, u32[]{:S(2)}, u32[]{:S(2)}) async-start(f32[16,8,128]{2,1,0:T(8,128)} %broadcast_in_dim.6), calls=%async_computation | async-start | bytes 131072 | tf_op jit(solution)/shard_map/all_to_all | solution.py:165
  16.2 16.5 %shard_map.93 = (bf16[4,8,48,512]{3,2,1,0:T(8,128)(2,1)}, bf16[4,8,48,512]{3,2,1,0:T(8,128)(2,1)}, f32[8,128]{1,0:T(8,128)}) custom-call(s32[1]{0:T(128)} %bitcast.5.core_ref, bf16[512,3072]{1,0:T(8,128)(2,1)} %query_ref.1, bf16[512,3072]{1,0:T(8,128)(2,1)} %grad_ref.1, f32[1,128]{1,0:T(1,128)} %bitcast.72), custom_call_target="tpu_custom_call" | custom-call | flops 60000000 | bytes 9500000 | tf_op jit(solution)/shard_map/pallas_call | solution.py:64
  32.8 2.6 convolution_convert_fusion
  35.4 1.9 collective-permute-start.2
  37.4 2.8 %collective-permute-done.2 = bf16[1536,384]{1,0:T(8,128)(2,1)S(1)} collective-permute-done((bf16[1536,384]{1,0:T(8,128)(2,1)S(1)}, bf16[1536,384]{1,0:T(8,128)(2,1)S(1)}, u32[]{:S(2)}, u32[]{:S(2)}) %collective-permute-start.2) | collective-permute-done | bytes 1179680 | tf_op jit(solution)/shard_map/ppermute | solution.py:180
  40.2 2.1 add_convert_fusion
  42.3 12.7 %all-to-all-start.1 = ((bf16[4,8,48,384]{3,2,1,0:T(8,128)(2,1)}), bf16[4,8,48,384]{3,2,1,0:T(8,128)(2,1)S(1)}, u32[]{:S(2)}, u32[]{:S(2)}) async-start(bf16[4,8,48,384]{3,2,1,0:T(8,128)(2,1)} %bitcast.21), calls=%async_computation.1 | async-start | bytes 2359296 | tf_op jit(solution)/shard_map/all_to_all | solution.py:165
  55.8 95.4 %all-gather.4.cloned.1.call-done = bf16[1536,384]{1,0:T(8,128)(2,1)} async-done(((bf16[48,384]{1,0:T(8,128)(2,1)}), bf16[1536,384]{1,0:T(8,128)(2,1)}) %all-gather.4.cloned.1.call-update) | async-done | bytes 1179664 | tf_op jit(solution)/shard_map/all_gather | solution.py:193
  151.2 1.4 slice_bitcast_fusion
  152.5 2.9 %collective-permute-start = (bf16[8,2,48,384]{3,2,1,0:T(8,128)(2,1)S(1)}, bf16[8,2,48,384]{3,2,1,0:T(8,128)(2,1)S(1)}, u32[]{:S(2)}, u32[]{:S(2)}) collective-permute-start(bf16[8,2,48,384]{3,2,1,0:T(8,128)(2,1)S(1)} %get-tuple-element.39.even_ref), channel_id=1, source_target_pairs={{32,0},{64,32},{96,64},{128,96},{160,128},{192,160},{224,192},{256... | collective-permute-start | bytes 1769480 | tf_op jit(solution)/shard_map/ppermute | solution.py:185
  155.5 3.1 %collective-permute-start.1 = (bf16[8,2,48,384]{3,2,1,0:T(8,128)(2,1)S(1)}, bf16[8,2,48,384]{3,2,1,0:T(8,128)(2,1)S(1)}, u32[]{:S(2)}, u32[]{:S(2)}) collective-permute-start(bf16[8,2,48,384]{3,2,1,0:T(8,128)(2,1)S(1)} %get-tuple-element.38.odd_ref), channel_id=1, source_target_pairs={{992,0},{0,32},{32,64},{64,96},{96,128},{128,160},{160,192},{192,2... | collective-permute-start | bytes 1769480 | tf_op jit(solution)/shard_map/ppermute | solution.py:185
  158.5 1.5 broadcast_in_dim.17.gain_ref
  160.0 1.2 reduce_sum.91
  162.5 4.3 %shard_map.94.first_ref = f32[384,512]{1,0:T(8,128)} custom-call(s32[2]{0:T(128)} %get-tuple-element.46.at_ref, bf16[8,2,48,384]{3,2,1,0:T(8,128)(2,1)} %copy-done.4, bf16[8,2,48,384]{3,2,1,0:T(8,128)(2,1)} %copy-done.3, bf16[4,8,48,512]{3,2,1,0:T(8,128)(2,1)} %get-tuple-element.10.query_own_ref, bf16[4,8,48,512]{3,2,1,0:T(8,128)(2,1)} %get-tuple-element.11.query_other_ref), custom_call_target="tpu_custom_call" | custom-call | flops 603979776 | bytes 4500000 | tf_op jit(solution)/shard_map/pallas_call | solution.py:146
  166.8 3.5 %collective-permute-done.even_ref = bf16[8,2,48,384]{3,2,1,0:T(8,128)(2,1)S(1)} collective-permute-done((bf16[8,2,48,384]{3,2,1,0:T(8,128)(2,1)S(1)}, bf16[8,2,48,384]{3,2,1,0:T(8,128)(2,1)S(1)}, u32[]{:S(2)}, u32[]{:S(2)}) %collective-permute-start) | collective-permute-done | bytes 589856 | tf_op jit(solution)/shard_map/ppermute | solution.py:185
  170.3 3.3 %collective-permute-done.1.odd_ref = bf16[8,2,48,384]{3,2,1,0:T(8,128)(2,1)S(1)} collective-permute-done((bf16[8,2,48,384]{3,2,1,0:T(8,128)(2,1)S(1)}, bf16[8,2,48,384]{3,2,1,0:T(8,128)(2,1)S(1)}, u32[]{:S(2)}, u32[]{:S(2)}) %collective-permute-start.1) | collective-permute-done | bytes 589856 | tf_op jit(solution)/shard_map/ppermute | solution.py:185
  174.4 5.1 %shard_map.95 = (f32[384,512]{1,0:T(8,128)}, f32[2,512]{1,0:T(2,128)}, f32[1,384]{1,0:T(1,128)}) custom-call(s32[2]{0:T(128)} %get-tuple-element.45.at_ref, bf16[8,2,48,384]{3,2,1,0:T(8,128)(2,1)} %copy-done.6, bf16[8,2,48,384]{3,2,1,0:T(8,128)(2,1)} %copy-done.7, bf16[4,8,48,512]{3,2,1,0:T(8,128)(2,1)} %get-tuple-element.10.query_own_ref, ...), custom_call_target="tpu_custom_call" | custom-call | flops 603979776 | bytes 4500000 | tf_op jit(solution)/shard_map/pallas_call | solution.py:146
  180.3 1.9 collective-permute-start.3
  184.0 14.3 %all-to-all-start.3 = ((f32[32,4,128]{2,1,0:T(4,128)}), f32[32,4,128]{2,1,0:T(4,128)S(1)}, u32[]{:S(2)}, u32[]{:S(2)}) async-start(f32[32,4,128]{2,1,0:T(4,128)} %broadcast_in_dim.16), calls=%async_computation.3 | async-start | bytes 131072 | tf_op jit(solution)/shard_map/all_to_all | solution.py:165
  199.2 24.1 %all-to-all-done.3 = f32[32,4,128]{2,1,0:T(4,128)S(1)} async-done(((f32[32,4,128]{2,1,0:T(4,128)}), f32[32,4,128]{2,1,0:T(4,128)S(1)}, u32[]{:S(2)}, u32[]{:S(2)}) %all-to-all-start.3) | async-done | bytes 65568 | tf_op jit(solution)/shard_map/all_to_all | solution.py:165
  223.4 3.4 %all-to-all-start.2 = ((bf16[8,48,384]{2,1,0:T(8,128)(2,1)}), bf16[8,48,384]{2,1,0:T(8,128)(2,1)S(1)}, u32[]{:S(2)}, u32[]{:S(2)}) async-start(bf16[8,48,384]{2,1,0:T(8,128)(2,1)} %reduce_sum.89), calls=%async_computation.2 | async-start | bytes 589824 | tf_op jit(solution)/shard_map/all_to_all | solution.py:165
  226.8 12.3 %all_gather.17 = f32[4,8,128]{2,1,0:T(8,128)S(1)} all-gather(f32[1,8,128]{2,1,0:T(8,128)S(1)} %all_gather_reshape.3), channel_id=1, replica_groups=mesh['far'=8,'high'=2,'low'=2,'core'=2,'x'=4,'y'=4] {'x'}, dimensions={0}, use_global_device_ids=true | all-gather | bytes 20480 | tf_op jit(solution)/shard_map/all_gather | solution.py:175
  239.1 12.3 %all-gather.1 = f32[32,128]{1,0:T(8,128)S(1)} all-gather(f32[8,128]{1,0:T(8,128)S(1)} %reduce_sum.87), channel_id=3, replica_groups=mesh['far'=8,'high'=2,'low'=2,'core'=2,'x'=4,'y'=4] {'y'}, dimensions={0}, use_global_device_ids=true | all-gather | bytes 20480 | tf_op jit(solution)/shard_map/all_gather | solution.py:175
  253.8 14.5 %all-to-all-done.2 = bf16[8,48,384]{2,1,0:T(8,128)(2,1)S(1)} async-done(((bf16[8,48,384]{2,1,0:T(8,128)(2,1)}), bf16[8,48,384]{2,1,0:T(8,128)(2,1)S(1)}, u32[]{:S(2)}, u32[]{:S(2)}) %all-to-all-start.2) | async-done | bytes 294944 | tf_op jit(solution)/shard_map/all_to_all | solution.py:165
  (53 shorter events, 11.3 us)
Async XLA Ops:
  8.3 31.9 %copy-start = (bf16[512,384]{0,1:T(8,128)(2,1)}, bf16[512,384]{0,1:T(8,128)(2,1)S(1)}, u32[]{:S(2)}) copy-start(bf16[512,384]{0,1:T(8,128)(2,1)S(1)} %copy.27) | copy-start | bytes 1179652
  9.2 23.6 %all-to-all-start = ((f32[16,8,128]{2,1,0:T(8,128)}), f32[16,8,128]{2,1,0:T(8,128)S(1)}, u32[]{:S(2)}, u32[]{:S(2)}) async-start(f32[16,8,128]{2,1,0:T(8,128)} %broadcast_in_dim.6), calls=%async_computation | async-start | bytes 131072 | tf_op jit(solution)/shard_map/all_to_all | solution.py:165
  16.2 16.6 %copy-start.10 = (f32[384]{0:T(512)S(1)}, f32[384]{0:T(512)}, u32[]{:S(2)}) copy-start(f32[384]{0:T(512)} %param.7) | copy-start | bytes 4612
  32.8 7.4 %copy-start.2 = (bf16[4,8,48,512]{3,2,1,0:T(8,128)(2,1)S(1)}, bf16[4,8,48,512]{3,2,1,0:T(8,128)(2,1)}, u32[]{:S(2)}) copy-start(bf16[4,8,48,512]{3,2,1,0:T(8,128)(2,1)} %get-tuple-element.10.query_own_ref) | copy-start | bytes 4718596
  35.4 4.7 %collective-permute-start.2 = (bf16[1536,384]{1,0:T(8,128)(2,1)S(1)}, bf16[1536,384]{1,0:T(8,128)(2,1)S(1)}, u32[]{:S(2)}, u32[]{:S(2)}) collective-permute-start(bf16[1536,384]{1,0:T(8,128)(2,1)S(1)} %convolution_convert_fusion), channel_id=1, source_target_pairs={{0,16},{16,0},{1,17},{17,1},{2,18},{18,2},{3,19},{19,3},{4,20},{20... | collective-permute-start | bytes 3538952 | tf_op jit(solution)/shard_map/ppermute | solution.py:180
  42.3 141.1 %all-to-all-start.1 = ((bf16[4,8,48,384]{3,2,1,0:T(8,128)(2,1)}), bf16[4,8,48,384]{3,2,1,0:T(8,128)(2,1)S(1)}, u32[]{:S(2)}, u32[]{:S(2)}) async-start(bf16[4,8,48,384]{3,2,1,0:T(8,128)(2,1)} %bitcast.21), calls=%async_computation.1 | async-start | bytes 2359296 | tf_op jit(solution)/shard_map/all_to_all | solution.py:165
  55.0 96.1 %all-gather.4.cloned.1.call-start = ((), (), s32[]{:S(2)}) async-start(), calls=%async_computation.4 | async-start | bytes 1216512 | tf_op jit(solution)/shard_map/all_gather | solution.py:193
  152.5 9.9 %copy-start.3 = (bf16[8,2,48,384]{3,2,1,0:T(8,128)(2,1)}, bf16[8,2,48,384]{3,2,1,0:T(8,128)(2,1)S(1)}, u32[]{:S(2)}) copy-start(bf16[8,2,48,384]{3,2,1,0:T(8,128)(2,1)S(1)} %get-tuple-element.38.odd_ref) | copy-start | bytes 1769476
  152.5 9.9 %copy-start.4 = (bf16[8,2,48,384]{3,2,1,0:T(8,128)(2,1)}, bf16[8,2,48,384]{3,2,1,0:T(8,128)(2,1)S(1)}, u32[]{:S(2)}) copy-start(bf16[8,2,48,384]{3,2,1,0:T(8,128)(2,1)S(1)} %get-tuple-element.39.even_ref) | copy-start | bytes 1769476
  152.5 17.8 %collective-permute-start = (bf16[8,2,48,384]{3,2,1,0:T(8,128)(2,1)S(1)}, bf16[8,2,48,384]{3,2,1,0:T(8,128)(2,1)S(1)}, u32[]{:S(2)}, u32[]{:S(2)}) collective-permute-start(bf16[8,2,48,384]{3,2,1,0:T(8,128)(2,1)S(1)} %get-tuple-element.39.even_ref), channel_id=1, source_target_pairs={{32,0},{64,32},{96,64},{128,96},{160,128},{192,160},{224,192},{256... | collective-permute-start | bytes 1769480 | tf_op jit(solution)/shard_map/ppermute | solution.py:185
  155.5 18.1 %collective-permute-start.1 = (bf16[8,2,48,384]{3,2,1,0:T(8,128)(2,1)S(1)}, bf16[8,2,48,384]{3,2,1,0:T(8,128)(2,1)S(1)}, u32[]{:S(2)}, u32[]{:S(2)}) collective-permute-start(bf16[8,2,48,384]{3,2,1,0:T(8,128)(2,1)S(1)} %get-tuple-element.38.odd_ref), channel_id=1, source_target_pairs={{992,0},{0,32},{32,64},{64,96},{96,128},{128,160},{160,192},{192,2... | collective-permute-start | bytes 1769480 | tf_op jit(solution)/shard_map/ppermute | solution.py:185
  170.3 3.3 %copy-start.6 = (bf16[8,2,48,384]{3,2,1,0:T(8,128)(2,1)}, bf16[8,2,48,384]{3,2,1,0:T(8,128)(2,1)S(1)}, u32[]{:S(2)}) copy-start(bf16[8,2,48,384]{3,2,1,0:T(8,128)(2,1)S(1)} %collective-permute-done.even_ref) | copy-start | bytes 1769476
  173.6 0.8 copy-start.7
  174.4 5.9 %copy-start.8 = (f32[128]{0:T(128)S(1)}, f32[128]{0:T(128)}, u32[]{:S(2)}) copy-start(f32[128]{0:T(128)} %reduce_sum.91) | copy-start | bytes 1540
  179.5 47.3 %copy-start.9 = (f32[2,512]{1,0:T(2,128)S(1)}, f32[2,512]{1,0:T(2,128)}, u32[]{:S(2)}) copy-start(f32[2,512]{1,0:T(2,128)} %get-tuple-element.13) | copy-start | bytes 12292
  179.5 72.0 %copy-start.1 = (bf16[512,384]{0,1:T(8,128)(2,1)S(1)}, bf16[512,384]{0,1:T(8,128)(2,1)}, u32[]{:S(2)}) copy-start(bf16[512,384]{0,1:T(8,128)(2,1)} %copy-done) | copy-start | bytes 1179652
  179.5 72.0 %copy-start.5 = (f32[384,512]{1,0:T(8,128)S(1)}, f32[384,512]{1,0:T(8,128)}, u32[]{:S(2)}) copy-start(f32[384,512]{1,0:T(8,128)} %get-tuple-element.12) | copy-start | bytes 2359300
  180.3 3.1 %collective-permute-start.3 = (f32[4,128]{1,0:T(4,128)S(1)}, f32[4,128]{1,0:T(4,128)S(1)}, u32[]{:S(2)}, u32[]{:S(2)}) collective-permute-start(f32[4,128]{1,0:T(4,128)S(1)} %maximum_bitcast_fusion), channel_id=1, source_target_pairs={{0,16},{16,0},{1,17},{17,1},{2,18},{18,2},{3,19},{19,3},{4,20},{20... | collective-permute-start | bytes 6152 | tf_op jit(solution)/shard_map/ppermute | solution.py:180
  184.0 39.3 %all-to-all-start.3 = ((f32[32,4,128]{2,1,0:T(4,128)}), f32[32,4,128]{2,1,0:T(4,128)S(1)}, u32[]{:S(2)}, u32[]{:S(2)}) async-start(f32[32,4,128]{2,1,0:T(4,128)} %broadcast_in_dim.16), calls=%async_computation.3 | async-start | bytes 131072 | tf_op jit(solution)/shard_map/all_to_all | solution.py:165
  223.4 44.9 %all-to-all-start.2 = ((bf16[8,48,384]{2,1,0:T(8,128)(2,1)}), bf16[8,48,384]{2,1,0:T(8,128)(2,1)S(1)}, u32[]{:S(2)}, u32[]{:S(2)}) async-start(bf16[8,48,384]{2,1,0:T(8,128)(2,1)} %reduce_sum.89), calls=%async_computation.2 | async-start | bytes 589824 | tf_op jit(solution)/shard_map/all_to_all | solution.py:165
Sparse Core Ops, SparseCore 0:
  58.5 92.5 all-gather.3

commit v2 on v0

--- a/solution.py
+++ b/solution.py
@@ -13,7 +13,7 @@
 FAR, NEAR = 8, 4
 COLS = 48
 MP = ("x", "y")
-DP = ("far", "near", "core")
+DP = ("far", "high", "low", "core")
 
 
 def qk_kernel(
@@ -89,17 +89,18 @@
 
 
 def input_kernel(
-    near_ref, own_ref, other_ref, query_own_ref, query_other_ref, x_ref, stat_ref, gain_ref,
+    core_ref, w_ref, query_own_ref, query_other_ref, x_ref, stat_ref, gain_ref,
     slope_ref, sums_ref, gains_ref, grad_ref,
 ):
+    core = core_ref[0]
     step = pl.program_id(0)
 
-    def product(w_ref, q_ref):
-        return lax.dot_general(
-            w_ref[...], q_ref[0], (((0,), (0,)), ((), ())), preferred_element_type=jnp.float32
-        )
-
-    part = product(own_ref, query_own_ref) + product(other_ref, query_other_ref)
+    def product(owner, q_ref):
+        w = w_ref[:, 0, owner].reshape(-1, w_ref.shape[-1])
+        q = q_ref[0].reshape(-1, q_ref.shape[-1])
+        return lax.dot_general(w, q, (((0,), (0,)), ((), ())), preferred_element_type=jnp.float32)
+
+    part = product(core, query_own_ref) + product(1 - core, query_other_ref)
 
     @pl.when(step == 0)
     def _():
@@ -122,41 +123,36 @@
         gains_ref[...] = jnp.sum(jnp.transpose(lanes), axis=0, keepdims=True)
 
 
-def input_backward(near, own, other, query_own, query_other, x, stat, gain):
+def input_backward(core, columns, query_own, query_other, x, stat, gain):
     rows, tokens = x.shape
-    span = own.shape[0] // NEAR
-    whole = lambda i, near: (0, 0)
+
+    def whole(shape):
+        return pl.BlockSpec(shape, lambda i, core: (0,) * len(shape))
+
+    query_spec = pl.BlockSpec((1, *query_own.shape[1:]), lambda i, core: (i, 0, 0, 0))
+    outs = ((rows, tokens), (2, tokens), (1, rows))
     return pl.pallas_call(
         input_kernel,
         grid_spec=pltpu.PrefetchScalarGridSpec(
             num_scalar_prefetch=1,
             grid=(NEAR,),
             in_specs=[
-                pl.BlockSpec((span, rows), lambda i, near: (i, 0)),
-                pl.BlockSpec((span, rows), lambda i, near: (i, 0)),
-                pl.BlockSpec((1, span, tokens), lambda i, near: ((near[0] + i) % NEAR, 0, 0)),
-                pl.BlockSpec((1, span, tokens), lambda i, near: ((near[0] + i) % NEAR, 0, 0)),
-                pl.BlockSpec((rows, tokens), whole),
-                pl.BlockSpec((2, tokens), whole),
-                pl.BlockSpec((rows, 1), whole),
+                pl.BlockSpec((FAR, 1, 2, COLS, rows), lambda i, core: (0, i, 0, 0, 0)),
+                query_spec,
+                query_spec,
+                whole(x.shape),
+                whole(stat.shape),
+                whole(gain.shape),
             ],
-            out_specs=[
-                pl.BlockSpec((rows, tokens), whole),
-                pl.BlockSpec((2, tokens), whole),
-                pl.BlockSpec((1, rows), whole),
-            ],
+            out_specs=[whole(o) for o in outs],
             scratch_shapes=[pltpu.VMEM((rows, tokens), jnp.float32)],
         ),
-        out_shape=[
-            jax.ShapeDtypeStruct((rows, tokens), jnp.float32),
-            jax.ShapeDtypeStruct((2, tokens), jnp.float32),
-            jax.ShapeDtypeStruct((1, rows), jnp.float32),
-        ],
+        out_shape=[jax.ShapeDtypeStruct(o, jnp.float32) for o in outs],
         compiler_params=pltpu.CompilerParams(dimension_semantics=("arbitrary",)),
         cost_estimate=pl.CostEstimate(
-            flops=2_400_000_000, bytes_accessed=7_000_000, transcendentals=0
+            flops=2 * 3072 * rows * tokens, bytes_accessed=7_000_000, transcendentals=0
         ),
-    )(near, own, other, query_own, query_other, x, stat, gain)
+    )(core, columns, query_own, query_other, x, stat, gain)
 
 
 def exchange(x, axes):
@@ -178,29 +174,17 @@
     return lax.ppermute(x, "core", [(0, 1), (1, 0)])
 
 
-def from_chip(x, distance):
-    chips = FAR * NEAR
-    return lax.ppermute(x, ("far", "near"), [((i + distance) % chips, i) for i in range(chips)])
-
-
 def shards(block_input, prenorm_gain, weight, query, grad_normed, qk_gain):
     tokens, rows = block_input.shape
     core = lax.axis_index("core").astype(jnp.int32).reshape(1)
-    near = lax.axis_index("near").astype(jnp.int32).reshape(1)
-
-    own = shared_by(weight.T, "far")
-    after = from_chip(own, 1)
-    before = from_chip(own, -1)
-    half = FAR // 2
-    across = [from_chip(own[:half], 2), from_chip(own[half:], -2)]
-    own = jnp.concatenate([own, after, *across, before]).reshape(-1, rows)
-    other = swapped(own)
+
+    columns = lax.all_gather(weight.T, DP, axis=0).reshape(FAR, NEAR, 2, COLS, rows)
 
     x_turned = block_input.T
     x = x_turned.astype(jnp.float32)
     sums = jnp.concatenate([jnp.sum(x, axis=0), jnp.sum(x * x, axis=0)]).reshape(8, 128)
-    sums = summed(sums, MP)
-    sums = sums.reshape(2, tokens)
+    sums = shared_by(sums, MP)
+    sums = jnp.sum(sums, axis=0).reshape(2, tokens)
 
     query_own, query_other, qk_partial = qk_backward(core, query, grad_normed, qk_gain)
 
@@ -220,25 +204,26 @@
     from_core = swapped(part)
     part = weight_part(query_own) + from_core.astype(jnp.float32)
     part = part.astype(jnp.bfloat16).reshape(NEAR, FAR, COLS, rows)
-    part = exchange(part, "near")
+    part = exchange(part, ("high", "low"))
     part = jnp.sum(part.astype(jnp.float32), axis=0).astype(jnp.bfloat16)
     part = exchange(part, "far")
     grad_weight = jnp.sum(part.astype(jnp.float32), axis=0).T
 
     slope, slopes, gains = input_backward(
-        near, own, other, query_own.reshape(NEAR, -1, tokens),
-        query_other.reshape(NEAR, -1, tokens), x_turned, jnp.concatenate([mean, inv]), gain,
+        core, columns, query_own, query_other, x_turned, jnp.concatenate([mean, inv]), gain
     )
     slopes = summed(slopes.reshape(8, 128), MP).reshape(2, tokens) / D
     input_gradient = (inv * (slope - slopes[0:1] - xhat * slopes[1:2])).astype(jnp.bfloat16).T
 
     gains = jnp.concatenate([gains[0], jnp.sum(qk_partial, axis=0)]).reshape(4, 128)
-    gains = summed(gains + swapped(gains), ("near", "far")).reshape(-1)
+    gains = gains + swapped(gains)
+    gains = shared_by(gains, ("far", "high", "low"))
+    gains = jnp.sum(gains, axis=0).reshape(-1)
     return (input_gradient, grad_weight, gains[:rows], gains[rows:])
 
 
 def solution(mesh):
-    finer = Mesh(mesh.devices.reshape(FAR, NEAR, 2, 4, 4), (*DP, *MP))
+    finer = Mesh(mesh.devices.reshape(FAR, 2, 2, 2, 4, 4), (*DP, *MP))
     in_specs = (P(DP, MP), P(MP), P(MP, DP), P(DP, None), P(DP, None), P())
     out_specs = (P(DP, MP), P(MP, DP), P(MP), P())
 

time: 248 us -> 296 us (1.19)
  the two profiles are of different devices: /device:TPU:8 before, /device:TPU:32 now
where the time goes in v2:
time: 296 us; the launch traced here: 295 us
  waiting for transfers between devices  179 us (60%)
  starting transfers between devices  41.3 us (14%)
  blocking collectives  24.7 us (8%)
  Pallas kernels  22.7 us (8%)
  between operations  14.2 us (5%)
  local copies, waits for them, and re-layouts  5.31 us (2%)
  matrix products  4.77 us (2%)
  other arithmetic  3.5 us (1%)
    all_gather x1, waiting for transfers between devices, shards(): lax.all_gather(weight.T, DP, axis=0).reshape(FAR, NEAR, 2, COLS, rows)  136 us
    all_to_all x4, waiting for transfers between devices, exchange(): return lax.all_to_all(x, axes, 0, 0, tiled=True)  38.6 us
    all_to_all x4, starting transfers between devices, exchange(): return lax.all_to_all(x, axes, 0, 0, tiled=True)  37.3 us
    all_gather x2, blocking collectives, summed(): x = jnp.sum(lax.all_gather(x, axis, axis=0), axis=0)  24.7 us
    pallas_call x1, Pallas kernels, qk_backward(): pl.pallas_call(qk_kernel, grid=(tokens // block,), in_specs=[pl.BlockSpec...  16.5 us
    pallas_call x1, Pallas kernels, input_backward(): pl.pallas_call(input_kernel, grid_spec=pltpu.PrefetchScalarGridSpec(num_s...  6.18 us
  transfers between devices with their start and end apart: 7, of which 5 were waited for; matrix products, arithmetic and copies ran while one was open for 2% of the time, Pallas kernels for 8%

profile of v2, /device:TPU:32, one launch (start us, length us, event | category | flops | bytes accessed | tf_op | source)
XLA Modules:
  0.0 295.4 jit_solution(13147471840400621926)
XLA Ops:
  7.2 1.2 copy.21
  9.2 7.0 %all-to-all-start = ((f32[16,8,128]{2,1,0:T(8,128)}), f32[16,8,128]{2,1,0:T(8,128)S(1)}, u32[]{:S(2)}, u32[]{:S(2)}) async-start(f32[16,8,128]{2,1,0:T(8,128)} %broadcast_in_dim.6), calls=%async_computation | async-start | bytes 131072 | tf_op jit(solution)/shard_map/all_to_all | solution.py:159
  16.2 16.5 %shard_map.93 = (bf16[4,8,48,512]{3,2,1,0:T(8,128)(2,1)}, bf16[4,8,48,512]{3,2,1,0:T(8,128)(2,1)}, f32[8,128]{1,0:T(8,128)}) custom-call(s32[1]{0:T(128)} %bitcast.5.core_ref, bf16[512,3072]{1,0:T(8,128)(2,1)} %query_ref.1, bf16[512,3072]{1,0:T(8,128)(2,1)} %grad_ref.1, f32[1,128]{1,0:T(1,128)} %bitcast.62), custom_call_target="tpu_custom_call" | custom-call | flops 60000000 | bytes 9500000 | tf_op jit(solution)/shard_map/pallas_call | solution.py:64
  32.8 2.6 convolution_convert_fusion
  35.4 1.9 collective-permute-start
  37.3 2.8 collective-permute-done
  40.1 2.2 add_convert_fusion
  42.3 12.8 %all-to-all-start.1 = ((bf16[4,8,48,384]{3,2,1,0:T(8,128)(2,1)}), bf16[4,8,48,384]{3,2,1,0:T(8,128)(2,1)S(1)}, u32[]{:S(2)}, u32[]{:S(2)}) async-start(bf16[4,8,48,384]{3,2,1,0:T(8,128)(2,1)} %bitcast.17), calls=%async_computation.1 | async-start | bytes 2359296 | tf_op jit(solution)/shard_map/all_to_all | solution.py:159
  55.1 0.7 all-gather.4.cloned.1.call-update
  55.8 0.8 broadcast_in_dim.17.gain_ref
  57.3 136.0 %all-gather.4.cloned.1.call-done = bf16[3072,384]{1,0:T(8,128)(2,1)} async-done(((bf16[48,384]{1,0:T(8,128)(2,1)}), bf16[3072,384]{1,0:T(8,128)(2,1)}) %all-gather.4.cloned.1.call-update) | async-done | bytes 2359312 | tf_op jit(solution)/shard_map/all_gather | solution.py:181
  193.2 6.2 %shard_map.94 = (f32[384,512]{1,0:T(8,128)}, f32[2,512]{1,0:T(2,128)}, f32[1,384]{1,0:T(1,128)}) custom-call(s32[1]{0:T(128)} %bitcast.5.core_ref, bf16[8,4,2,48,384]{4,3,2,1,0:T(8,128)(2,1)} %bitcast.52, bf16[4,8,48,512]{3,2,1,0:T(8,128)(2,1)} %get-tuple-element.10.query_own_ref, bf16[4,8,48,512]{3,2,1,0:T(8,128)(2,1)} %get-tuple-element.11.query_other_ref, ...), custom_call_target="tpu_custom_call" | custom-call | flops 1207959552 | bytes 7000000 | tf_op jit(solution)/shard_map/pallas_call | solution.py:134
  199.4 0.8 reduce.1
  200.2 2.1 collective-permute-start.1
  202.4 0.9 collective-permute-done.1
  203.9 14.0 %all-to-all-start.3 = ((f32[32,4,128]{2,1,0:T(4,128)}), f32[32,4,128]{2,1,0:T(4,128)S(1)}, u32[]{:S(2)}, u32[]{:S(2)}) async-start(f32[32,4,128]{2,1,0:T(4,128)} %broadcast_in_dim.16), calls=%async_computation.3 | async-start | bytes 131072 | tf_op jit(solution)/shard_map/all_to_all | solution.py:159
  217.9 0.9 reduce_sum.89
  218.9 24.2 %all-to-all-done.3 = f32[32,4,128]{2,1,0:T(4,128)S(1)} async-done(((f32[32,4,128]{2,1,0:T(4,128)}), f32[32,4,128]{2,1,0:T(4,128)S(1)}, u32[]{:S(2)}, u32[]{:S(2)}) %all-to-all-start.3) | async-done | bytes 65568 | tf_op jit(solution)/shard_map/all_to_all | solution.py:159
  243.0 3.4 %all-to-all-start.2 = ((bf16[8,48,384]{2,1,0:T(8,128)(2,1)}), bf16[8,48,384]{2,1,0:T(8,128)(2,1)S(1)}, u32[]{:S(2)}, u32[]{:S(2)}) async-start(bf16[8,48,384]{2,1,0:T(8,128)(2,1)} %reduce_sum.89), calls=%async_computation.2 | async-start | bytes 589824 | tf_op jit(solution)/shard_map/all_to_all | solution.py:159
  246.5 12.3 %all_gather.17 = f32[4,8,128]{2,1,0:T(8,128)S(1)} all-gather(f32[1,8,128]{2,1,0:T(8,128)S(1)} %all_gather_reshape.3), channel_id=1, replica_groups=mesh['far'=8,'high'=2,'low'=2,'core'=2,'x'=4,'y'=4] {'x'}, dimensions={0}, use_global_device_ids=true | all-gather | bytes 20480 | tf_op jit(solution)/shard_map/all_gather | solution.py:169
  258.8 12.3 %all-gather.1 = f32[32,128]{1,0:T(8,128)S(1)} all-gather(f32[8,128]{1,0:T(8,128)S(1)} %reduce_sum.87), channel_id=3, replica_groups=mesh['far'=8,'high'=2,'low'=2,'core'=2,'x'=4,'y'=4] {'y'}, dimensions={0}, use_global_device_ids=true | all-gather | bytes 20480 | tf_op jit(solution)/shard_map/all_gather | solution.py:169
  271.4 0.9 copy.24
  273.5 14.4 %all-to-all-done.2 = bf16[8,48,384]{2,1,0:T(8,128)(2,1)S(1)} async-done(((bf16[8,48,384]{2,1,0:T(8,128)(2,1)}), bf16[8,48,384]{2,1,0:T(8,128)(2,1)S(1)}, u32[]{:S(2)}, u32[]{:S(2)}) %all-to-all-start.2) | async-done | bytes 294944 | tf_op jit(solution)/shard_map/all_to_all | solution.py:159
  287.9 0.7 convert_reduce_fusion.1
  (38 shorter events, 3.5 us)
Async XLA Ops:
  8.3 31.8 %copy-start = (bf16[512,384]{0,1:T(8,128)(2,1)}, bf16[512,384]{0,1:T(8,128)(2,1)S(1)}, u32[]{:S(2)}) copy-start(bf16[512,384]{0,1:T(8,128)(2,1)S(1)} %copy.21) | copy-start | bytes 1179652
  9.2 23.6 %all-to-all-start = ((f32[16,8,128]{2,1,0:T(8,128)}), f32[16,8,128]{2,1,0:T(8,128)S(1)}, u32[]{:S(2)}, u32[]{:S(2)}) async-start(f32[16,8,128]{2,1,0:T(8,128)} %broadcast_in_dim.6), calls=%async_computation | async-start | bytes 131072 | tf_op jit(solution)/shard_map/all_to_all | solution.py:159
  16.2 16.6 %copy-start.6 = (f32[384]{0:T(512)S(1)}, f32[384]{0:T(512)}, u32[]{:S(2)}) copy-start(f32[384]{0:T(512)} %param.7) | copy-start | bytes 4612
  32.8 7.4 %copy-start.2 = (bf16[4,8,48,512]{3,2,1,0:T(8,128)(2,1)S(1)}, bf16[4,8,48,512]{3,2,1,0:T(8,128)(2,1)}, u32[]{:S(2)}) copy-start(bf16[4,8,48,512]{3,2,1,0:T(8,128)(2,1)} %get-tuple-element.10.query_own_ref) | copy-start | bytes 4718596
  35.4 4.7 %collective-permute-start = (bf16[1536,384]{1,0:T(8,128)(2,1)S(1)}, bf16[1536,384]{1,0:T(8,128)(2,1)S(1)}, u32[]{:S(2)}, u32[]{:S(2)}) collective-permute-start(bf16[1536,384]{1,0:T(8,128)(2,1)S(1)} %convolution_convert_fusion), channel_id=1, source_target_pairs={{0,16},{16,0},{1,17},{17,1},{2,18},{18,2},{3,19},{19,3},{4,20},{20... | collective-permute-start | bytes 3538952 | tf_op jit(solution)/shard_map/ppermute | solution.py:174
  42.3 14.3 %copy-start.4 = (f32[8,128]{1,0:T(8,128)S(1)}, f32[8,128]{1,0:T(8,128)}, u32[]{:S(2)}) copy-start(f32[8,128]{1,0:T(8,128)} %get-tuple-element.15) | copy-start | bytes 12292
  42.3 161.0 %all-to-all-start.1 = ((bf16[4,8,48,384]{3,2,1,0:T(8,128)(2,1)}), bf16[4,8,48,384]{3,2,1,0:T(8,128)(2,1)S(1)}, u32[]{:S(2)}, u32[]{:S(2)}) async-start(bf16[4,8,48,384]{3,2,1,0:T(8,128)(2,1)} %bitcast.17), calls=%async_computation.1 | async-start | bytes 2359296 | tf_op jit(solution)/shard_map/all_to_all | solution.py:159
  55.1 138.1 %all-gather.4.cloned.1.call-start = ((), (), s32[]{:S(2)}) async-start(), calls=%async_computation.4 | async-start | bytes 2396160 | tf_op jit(solution)/shard_map/all_gather | solution.py:181
  199.4 47.1 %copy-start.5 = (f32[2,512]{1,0:T(2,128)S(1)}, f32[2,512]{1,0:T(2,128)}, u32[]{:S(2)}) copy-start(f32[2,512]{1,0:T(2,128)} %get-tuple-element.13) | copy-start | bytes 12292
  199.4 71.8 %copy-start.1 = (bf16[512,384]{0,1:T(8,128)(2,1)S(1)}, bf16[512,384]{0,1:T(8,128)(2,1)}, u32[]{:S(2)}) copy-start(bf16[512,384]{0,1:T(8,128)(2,1)} %copy-done) | copy-start | bytes 1179652
  199.4 71.8 %copy-start.3 = (f32[384,512]{1,0:T(8,128)S(1)}, f32[384,512]{1,0:T(8,128)}, u32[]{:S(2)}) copy-start(f32[384,512]{1,0:T(8,128)} %get-tuple-element.12) | copy-start | bytes 2359300
  200.2 3.1 %collective-permute-start.1 = (f32[4,128]{1,0:T(4,128)S(1)}, f32[4,128]{1,0:T(4,128)S(1)}, u32[]{:S(2)}, u32[]{:S(2)}) collective-permute-start(f32[4,128]{1,0:T(4,128)S(1)} %maximum_bitcast_fusion), channel_id=1, source_target_pairs={{0,16},{16,0},{1,17},{17,1},{2,18},{18,2},{3,19},{19,3},{4,20},{20... | collective-permute-start | bytes 6152 | tf_op jit(solution)/shard_map/ppermute | solution.py:174
  203.9 39.1 %all-to-all-start.3 = ((f32[32,4,128]{2,1,0:T(4,128)}), f32[32,4,128]{2,1,0:T(4,128)S(1)}, u32[]{:S(2)}, u32[]{:S(2)}) async-start(f32[32,4,128]{2,1,0:T(4,128)} %broadcast_in_dim.16), calls=%async_computation.3 | async-start | bytes 131072 | tf_op jit(solution)/shard_map/all_to_all | solution.py:159
  243.0 44.8 %all-to-all-start.2 = ((bf16[8,48,384]{2,1,0:T(8,128)(2,1)}), bf16[8,48,384]{2,1,0:T(8,128)(2,1)S(1)}, u32[]{:S(2)}, u32[]{:S(2)}) async-start(bf16[8,48,384]{2,1,0:T(8,128)(2,1)} %reduce_sum.89), calls=%async_computation.2 | async-start | bytes 589824 | tf_op jit(solution)/shard_map/all_to_all | solution.py:159
Sparse Core Ops, SparseCore 0:
  58.6 134.5 all-gather.3

commit v3 on v1

--- a/solution.py
+++ b/solution.py
@@ -88,20 +88,20 @@
     )(core, query, grad_normed, qk_gain.reshape(1, HEAD))
 
 
-def set_product(core, query_own_ref, query_other_ref):
+def set_product(query_own_ref, query_other_ref):
     def product(w_ref, owner, q_ref):
         w = w_ref[:, owner].reshape(-1, w_ref.shape[-1])
         q = q_ref[0].reshape(-1, q_ref.shape[-1])
         return lax.dot_general(w, q, (((0,), (0,)), ((), ())), preferred_element_type=jnp.float32)
 
     def both(w_ref):
-        return product(w_ref, core, query_own_ref) + product(w_ref, 1 - core, query_other_ref)
+        return product(w_ref, 0, query_own_ref) + product(w_ref, 1, query_other_ref)
 
     return both
 
 
 def first_kernel(at_ref, even_ref, odd_ref, query_own_ref, query_other_ref, out_ref):
-    both = set_product(at_ref[0], query_own_ref, query_other_ref)
+    both = set_product(query_own_ref, query_other_ref)
 
     @pl.when(pl.program_id(0) == 0)
     def _():
@@ -116,7 +116,7 @@
     at_ref, even_ref, odd_ref, query_own_ref, query_other_ref, first_ref, x_ref, stat_ref, gain_ref,
     slope_ref, sums_ref, gains_ref, grad_ref,
 ):
-    both = set_product(at_ref[0], query_own_ref, query_other_ref)
+    both = set_product(query_own_ref, query_other_ref)
 
     @pl.when(pl.program_id(0) == 0)
     def _():
@@ -142,7 +142,7 @@
     def whole(shape):
         return pl.BlockSpec(shape, lambda i, at: (0,) * len(shape))
 
-    query_spec = pl.BlockSpec((1, *span), lambda i, at: (2 * i + at[1], 0, 0, 0))
+    query_spec = pl.BlockSpec((1, *span), lambda i, at: (2 * i + at[0], 0, 0, 0))
     return pl.pallas_call(
         body,
         grid_spec=pltpu.PrefetchScalarGridSpec(
@@ -170,6 +170,12 @@
     return exchange(copies, axes)
 
 
+def thirds(x):
+    high = lax.reduce_precision(x, 8, 7)
+    middle = lax.reduce_precision(x - high, 8, 7)
+    return jnp.stack([high, middle, x - high - middle]).astype(jnp.bfloat16)
+
+
 def summed(x, axes):
     for axis in axes:
         x = jnp.sum(lax.all_gather(x, axis, axis=0), axis=0)
@@ -188,10 +194,11 @@
 def shards(block_input, prenorm_gain, weight, query, grad_normed, qk_gain):
     tokens, rows = block_input.shape
     core = lax.axis_index("core").astype(jnp.int32)
-    parity = lax.axis_index("low").astype(jnp.int32)
-
-    mine = lax.all_gather(weight.T, ("far", "high", "core"), axis=0)
-    mine = mine.reshape(FAR, 2, 2, COLS, rows)
+    parity = lax.axis_index("low").astype(jnp.int32).reshape(1)
+
+    mine = weight.T
+    mine = jnp.stack([mine, swapped(mine)])
+    mine = lax.all_gather(mine, ("far", "high"), axis=0).reshape(FAR, 2, 2, COLS, rows)
     even, odd = mine[:, 0], mine[:, 1]
     theirs_even = from_chip(even, 1)
     theirs_odd = from_chip(odd, -1)
@@ -222,25 +229,28 @@
     part = part.astype(jnp.bfloat16).reshape(NEAR, FAR, COLS, rows)
     part = exchange(part, ("high", "low"))
     part = jnp.sum(part.astype(jnp.float32), axis=0).astype(jnp.bfloat16)
-    part = exchange(part, "far")
-    grad_weight = jnp.sum(part.astype(jnp.float32), axis=0).T
 
     (first,) = input_part(
-        first_kernel, jnp.stack([core, parity]), even, odd, query_own, query_other,
+        first_kernel, parity, even, odd, query_own, query_other,
         (), ((rows, tokens),), (),
     )
     slope, slopes, gains = input_part(
-        input_kernel, jnp.stack([core, 1 - parity]), theirs_even, theirs_odd,
+        input_kernel, 1 - parity, theirs_even, theirs_odd,
         query_own, query_other, (first, x_turned, jnp.concatenate([mean, inv]), gain),
         ((rows, tokens), (2, tokens), (1, rows)), (pltpu.VMEM((rows, tokens), jnp.float32),),
     )
     slopes = summed(slopes.reshape(8, 128), MP).reshape(2, tokens) / D
     input_gradient = (inv * (slope - slopes[0:1] - xhat * slopes[1:2])).astype(jnp.bfloat16).T
 
-    gains = jnp.concatenate([gains[0], jnp.sum(qk_partial, axis=0)]).reshape(4, 128)
-    gains = gains + swapped(gains)
-    gains = shared_by(gains, ("far", "high", "low"))
-    gains = jnp.sum(gains, axis=0).reshape(-1)
+    gains = jnp.concatenate([gains[0], jnp.sum(qk_partial, axis=0)])
+    gains = gains + swapped(gains.reshape(4, 128)).reshape(-1)
+    rest = jnp.pad(thirds(gains).reshape(-1, rows), ((0, 4), (0, 0)))
+    part = jnp.concatenate([part, jnp.broadcast_to(rest[None], (FAR, *rest.shape))], axis=1)
+    part = exchange(part, "far")
+    part = jnp.sum(part.astype(jnp.float32), axis=0)
+    grad_weight = part[:COLS].T
+    gains = jnp.sum(part[COLS : COLS + 4].reshape(3, 4, 128), axis=0)
+    gains = jnp.sum(lax.all_gather(gains, ("high", "low"), axis=0), axis=0).reshape(-1)
     return (input_gradient, grad_weight, gains[:rows], gains[rows:])
 
 

time: 276 us -> 258 us (0.935)
  waiting for transfers between devices: 145 us -> 123 us
  blocking collectives: 24.6 us -> 35.3 us
  starting transfers between devices: 47.2 us -> 42.2 us
    all_to_all x4 -> x3, waiting for transfers between devices: 38.6 us -> 21 us  [exchange(): return lax.all_to_all(x, axes, 0, 0, tiled=True)]
    all_gather x0 -> x1, blocking collectives: none -> 10.5 us  [shards(): lax.all_gather(gains, ('high', 'low'), axis=0)]
    all_to_all x4 -> x3, starting transfers between devices: 37.4 us -> 30.6 us  [exchange(): return lax.all_to_all(x, axes, 0, 0, tiled=True)]
    ppermute x2, waiting for transfers between devices: 6.82 us -> 2.1 us  [from_chip(): lax.ppermute(x, ('far', 'high', 'low'), [((i + distance) % chips, i) for...]
    ppermute x2 -> x3, starting transfers between devices: 3.84 us -> 5.75 us  [swapped(): return lax.ppermute(x, 'core', [(0, 1), (1, 0)])]
  transfers between devices with their start and end apart: 9 -> 9, of which waited for: 7 -> 6; matrix products, arithmetic and copies ran while one was open for 3% -> 3% of each run, Pallas kernels for 9% -> 9%
where the time goes in v3:
time: 258 us
  waiting for transfers between devices  123 us (48%)
  starting transfers between devices  42.2 us (16%)
  blocking collectives  35.3 us (14%)
  Pallas kernels  24.3 us (9%)
  between operations  14.3 us (6%)
  local copies, waits for them, and re-layouts  8.26 us (3%)
  other arithmetic  5.41 us (2%)
  matrix products  4.76 us (2%)
    all_gather x1, waiting for transfers between devices, shards(): lax.all_gather(mine, ('far', 'high'), axis=0).reshape(FAR, 2, 2, COLS, rows)  94.9 us
    all_to_all x3, starting transfers between devices, exchange(): return lax.all_to_all(x, axes, 0, 0, tiled=True)  30.6 us
    all_gather x2, blocking collectives, summed(): x = jnp.sum(lax.all_gather(x, axis, axis=0), axis=0)  24.8 us
    all_to_all x3, waiting for transfers between devices, exchange(): return lax.all_to_all(x, axes, 0, 0, tiled=True)  21 us
    pallas_call x1, Pallas kernels, qk_backward(): pl.pallas_call(qk_kernel, grid=(tokens // block,), in_specs=[pl.BlockSpec...  16.5 us
    all_gather x1, blocking collectives, shards(): lax.all_gather(gains, ('high', 'low'), axis=0)  10.5 us
    pallas_call x2, Pallas kernels, input_part(): pl.pallas_call(body, grid_spec=pltpu.PrefetchScalarGridSpec(num_scalar_pr...  7.85 us
    ppermute x2, starting transfers between devices, from_chip(): lax.ppermute(x, ('far', 'high', 'low'), [((i + distance) % chips, i) for...  5.84 us
  transfers between devices with their start and end apart: 9, of which 6 were waited for; matrix products, arithmetic and copies ran while one was open for 3% of the time, Pallas kernels for 9%

profile of v3, /device:TPU:32, one launch (start us, length us, event | category | flops | bytes accessed | tf_op | source)
XLA Modules:
  0.0 257.7 jit_solution(7361845977880984520)
XLA Ops:
  9.2 7.0 %all-to-all-start = ((f32[16,8,128]{2,1,0:T(8,128)}), f32[16,8,128]{2,1,0:T(8,128)S(1)}, u32[]{:S(2)}, u32[]{:S(2)}) async-start(f32[16,8,128]{2,1,0:T(8,128)} %broadcast_in_dim.6), calls=%async_computation | async-start | bytes 131072 | tf_op jit(solution)/shard_map/all_to_all | solution.py:165
  16.2 16.5 %shard_map.93 = (bf16[4,8,48,512]{3,2,1,0:T(8,128)(2,1)}, bf16[4,8,48,512]{3,2,1,0:T(8,128)(2,1)}, f32[8,128]{1,0:T(8,128)}) custom-call(s32[1]{0:T(128)} %bitcast.12.core_ref, bf16[512,3072]{1,0:T(8,128)(2,1)} %query_ref.1, bf16[512,3072]{1,0:T(8,128)(2,1)} %grad_ref.1, f32[1,128]{1,0:T(1,128)} %bitcast.80), custom_call_target="tpu_custom_call" | custom-call | flops 60000000 | bytes 9500000 | tf_op jit(solution)/shard_map/pallas_call | solution.py:64
  32.8 2.6 %convolution_convert_fusion = bf16[1536,384]{1,0:T(8,128)(2,1)S(1)} fusion(bf16[1536,512]{1,0:T(8,128)(2,1)} %bitcast.67, f32[384]{0:T(512)S(1)} %copy-done.11, f32[512]{0:T(512)S(1)} %get-tuple-element.40, f32[512]{0:T(512)S(1)} %fusion.16, bf16[512,384]{0,1:T(8,128)(2,1)S(1)} %copy.22), kind=kOutput, calls=%fused_computation | convolution fusion | flops 605552640 | bytes 3151360 | tf_op jit(solution)/shard_map/dot_general | solution.py:221
  35.4 1.9 collective-permute-start.3
  37.3 2.8 %collective-permute-done.3 = bf16[1536,384]{1,0:T(8,128)(2,1)S(1)} collective-permute-done((bf16[1536,384]{1,0:T(8,128)(2,1)S(1)}, bf16[1536,384]{1,0:T(8,128)(2,1)S(1)}, u32[]{:S(2)}, u32[]{:S(2)}) %collective-permute-start.3) | collective-permute-done | bytes 1179680 | tf_op jit(solution)/shard_map/ppermute | solution.py:186
  40.1 2.1 add_convert_fusion
  42.3 12.8 %all-to-all-start.1 = ((bf16[4,8,48,384]{3,2,1,0:T(8,128)(2,1)}), bf16[4,8,48,384]{3,2,1,0:T(8,128)(2,1)S(1)}, u32[]{:S(2)}, u32[]{:S(2)}) async-start(bf16[4,8,48,384]{3,2,1,0:T(8,128)(2,1)} %bitcast.22), calls=%async_computation.1 | async-start | bytes 2359296 | tf_op jit(solution)/shard_map/all_to_all | solution.py:165
  55.1 1.9 collective-permute-start
  57.0 1.2 collective-permute-done
  58.9 94.9 %all-gather.6.cloned.1.call-done = bf16[32,48,384]{2,1,0:T(8,128)(2,1)} async-done(((bf16[2,48,384]{2,1,0:T(8,128)(2,1)}), bf16[32,48,384]{2,1,0:T(8,128)(2,1)}) %all-gather.6.cloned.1.call-update) | async-done | bytes 1179664 | tf_op jit(solution)/shard_map/all_gather | solution.py:201
  153.8 1.4 slice_bitcast_fusion
  155.1 2.3 collective-permute-start.1
  157.4 3.6 %collective-permute-start.2 = (bf16[8,2,48,384]{3,2,1,0:T(8,128)(2,1)S(1)}, bf16[8,2,48,384]{3,2,1,0:T(8,128)(2,1)S(1)}, u32[]{:S(2)}, u32[]{:S(2)}) collective-permute-start(bf16[8,2,48,384]{3,2,1,0:T(8,128)(2,1)S(1)} %get-tuple-element.36.odd_ref), channel_id=1, source_target_pairs={{992,0},{0,32},{32,64},{64,96},{96,128},{128,160},{160,192},{192,2... | collective-permute-start | bytes 1769480 | tf_op jit(solution)/shard_map/ppermute | solution.py:191
  161.0 1.5 broadcast_in_dim.17.gain_ref
  162.5 1.2 reduce_sum.99
  164.3 3.6 %shard_map.94.first_ref = f32[384,512]{1,0:T(8,128)} custom-call(s32[1]{0:T(128)} %bitcast.5.at_ref, bf16[8,2,48,384]{3,2,1,0:T(8,128)(2,1)} %copy-done.4, bf16[8,2,48,384]{3,2,1,0:T(8,128)(2,1)} %copy-done.3, bf16[4,8,48,512]{3,2,1,0:T(8,128)(2,1)} %get-tuple-element.10.query_own_ref, bf16[4,8,48,512]{3,2,1,0:T(8,128)(2,1)} %get-tuple-element.11.query_other_ref), custom_call_target="tpu_custom_call" | custom-call | flops 603979776 | bytes 4500000 | tf_op jit(solution)/shard_map/pallas_call | solution.py:146
  167.9 2.1 collective-permute-done.2.odd_ref
  170.8 4.2 %shard_map.95 = (f32[384,512]{1,0:T(8,128)}, f32[2,512]{1,0:T(2,128)}, f32[1,384]{1,0:T(1,128)}) custom-call(s32[1]{0:T(128)S(6)} %sub.64.at_ref, bf16[8,2,48,384]{3,2,1,0:T(8,128)(2,1)} %copy-done.6, bf16[8,2,48,384]{3,2,1,0:T(8,128)(2,1)} %copy-done.7, bf16[4,8,48,512]{3,2,1,0:T(8,128)(2,1)} %get-tuple-element.10.query_own_ref, ...), custom_call_target="tpu_custom_call" | custom-call | flops 603979776 | bytes 4500000 | tf_op jit(solution)/shard_map/pallas_call | solution.py:146
  175.9 1.9 collective-permute-start.4
  180.7 10.8 %all-to-all-start.2 = ((bf16[8,56,384]{2,1,0:T(8,128)(2,1)}), bf16[8,56,384]{2,1,0:T(8,128)(2,1)S(1)}, u32[]{:S(2)}, u32[]{:S(2)}) async-start(bf16[8,56,384]{2,1,0:T(8,128)(2,1)} %pad_maximum_fusion), calls=%async_computation.2 | async-start | bytes 688128 | tf_op jit(solution)/shard_map/all_to_all | solution.py:165
  191.5 12.5 %all_gather.23 = f32[4,8,128]{2,1,0:T(8,128)S(1)} all-gather(f32[1,8,128]{2,1,0:T(8,128)S(1)} %all_gather_reshape.3), channel_id=1, replica_groups=mesh['far'=8,'high'=2,'low'=2,'core'=2,'x'=4,'y'=4] {'x'}, dimensions={0}, use_global_device_ids=true | all-gather | bytes 20480 | tf_op jit(solution)/shard_map/all_gather | solution.py:181
  204.0 12.3 %all-gather.1 = f32[32,128]{1,0:T(8,128)S(1)} all-gather(f32[8,128]{1,0:T(8,128)S(1)} %reduce_sum.96), channel_id=3, replica_groups=mesh['far'=8,'high'=2,'low'=2,'core'=2,'x'=4,'y'=4] {'y'}, dimensions={0}, use_global_device_ids=true | all-gather | bytes 20480 | tf_op jit(solution)/shard_map/all_gather | solution.py:181
  217.5 21.0 %all-to-all-done.2 = bf16[8,56,384]{2,1,0:T(8,128)(2,1)S(1)} async-done(((bf16[8,56,384]{2,1,0:T(8,128)(2,1)}), bf16[8,56,384]{2,1,0:T(8,128)(2,1)S(1)}, u32[]{:S(2)}, u32[]{:S(2)}) %all-to-all-start.2) | async-done | bytes 344096 | tf_op jit(solution)/shard_map/all_to_all | solution.py:165
  239.2 10.5 %all-gather.3 = f32[4,4,128]{2,1,0:T(4,128)S(1)} all-gather(f32[1,4,128]{2,1,0:T(4,128)S(1)} %bitcast.77), channel_id=4, replica_groups=mesh['far'=8,'high'=2,'low'=2,'core'=2,'x'=4,'y'=4] {'high','low'}, dimensions={0}, use_global_device_ids=true | all-gather | bytes 10240 | tf_op jit(solution)/shard_map/all_gather | solution.py:253
  (65 shorter events, 10.8 us)
Async XLA Ops:
  8.3 31.8 %copy-start = (bf16[512,384]{0,1:T(8,128)(2,1)}, bf16[512,384]{0,1:T(8,128)(2,1)S(1)}, u32[]{:S(2)}) copy-start(bf16[512,384]{0,1:T(8,128)(2,1)S(1)} %copy.22) | copy-start | bytes 1179652
  9.2 23.6 %all-to-all-start = ((f32[16,8,128]{2,1,0:T(8,128)}), f32[16,8,128]{2,1,0:T(8,128)S(1)}, u32[]{:S(2)}, u32[]{:S(2)}) async-start(f32[16,8,128]{2,1,0:T(8,128)} %broadcast_in_dim.6), calls=%async_computation | async-start | bytes 131072 | tf_op jit(solution)/shard_map/all_to_all | solution.py:165
  16.2 16.6 %copy-start.11 = (f32[384]{0:T(512)S(1)}, f32[384]{0:T(512)}, u32[]{:S(2)}) copy-start(f32[384]{0:T(512)} %param.7) | copy-start | bytes 4612
  32.8 7.4 %copy-start.2 = (bf16[4,8,48,512]{3,2,1,0:T(8,128)(2,1)S(1)}, bf16[4,8,48,512]{3,2,1,0:T(8,128)(2,1)}, u32[]{:S(2)}) copy-start(bf16[4,8,48,512]{3,2,1,0:T(8,128)(2,1)} %get-tuple-element.10.query_own_ref) | copy-start | bytes 4718596
  35.4 4.7 %collective-permute-start.3 = (bf16[1536,384]{1,0:T(8,128)(2,1)S(1)}, bf16[1536,384]{1,0:T(8,128)(2,1)S(1)}, u32[]{:S(2)}, u32[]{:S(2)}) collective-permute-start(bf16[1536,384]{1,0:T(8,128)(2,1)S(1)} %convolution_convert_fusion), channel_id=1, source_target_pairs={{0,16},{16,0},{1,17},{17,1},{2,18},{18,2},{3,19},{19,3},{4,20},{20... | collective-permute-start | bytes 3538952 | tf_op jit(solution)/shard_map/ppermute | solution.py:186
  42.3 12.8 %copy-start.8 = (bf16[384,48]{0,1:T(8,128)(2,1)S(1)}, bf16[384,48]{0,1:T(8,128)(2,1)}, u32[]{:S(2)}) copy-start(bf16[384,48]{0,1:T(8,128)(2,1)} %param.8) | copy-start | bytes 110596
  42.3 137.4 %all-to-all-start.1 = ((bf16[4,8,48,384]{3,2,1,0:T(8,128)(2,1)}), bf16[4,8,48,384]{3,2,1,0:T(8,128)(2,1)S(1)}, u32[]{:S(2)}, u32[]{:S(2)}) async-start(bf16[4,8,48,384]{3,2,1,0:T(8,128)(2,1)} %bitcast.22), calls=%async_computation.1 | async-start | bytes 2359296 | tf_op jit(solution)/shard_map/all_to_all | solution.py:165
  55.1 98.6 %all-gather.6.cloned.1.call-start = ((), (), s32[]{:S(2)}) async-start(), calls=%async_computation.3 | async-start | bytes 1253376 | tf_op jit(solution)/shard_map/all_gather | solution.py:201
  55.1 3.1 %collective-permute-start = (bf16[48,384]{1,0:T(8,128)(2,1)S(1)}, bf16[48,384]{1,0:T(8,128)(2,1)S(1)}, u32[]{:S(2)}, u32[]{:S(2)}) collective-permute-start(bf16[48,384]{1,0:T(8,128)(2,1)S(1)} %bitcast.69), channel_id=1, source_target_pairs={{0,16},{16,0},{1,17},{17,1},{2,18},{18,2},{3,19},{19,3},{4,20},{20... | collective-permute-start | bytes 110600 | tf_op jit(solution)/shard_map/ppermute | solution.py:186
  155.1 9.1 %copy-start.3 = (bf16[8,2,48,384]{3,2,1,0:T(8,128)(2,1)}, bf16[8,2,48,384]{3,2,1,0:T(8,128)(2,1)S(1)}, u32[]{:S(2)}) copy-start(bf16[8,2,48,384]{3,2,1,0:T(8,128)(2,1)S(1)} %get-tuple-element.36.odd_ref) | copy-start | bytes 1769476
  155.1 9.1 %copy-start.4 = (bf16[8,2,48,384]{3,2,1,0:T(8,128)(2,1)}, bf16[8,2,48,384]{3,2,1,0:T(8,128)(2,1)S(1)}, u32[]{:S(2)}) copy-start(bf16[8,2,48,384]{3,2,1,0:T(8,128)(2,1)S(1)} %get-tuple-element.37.even_ref) | copy-start | bytes 1769476
  155.1 12.8 %collective-permute-start.1 = (bf16[8,2,48,384]{3,2,1,0:T(8,128)(2,1)S(1)}, bf16[8,2,48,384]{3,2,1,0:T(8,128)(2,1)S(1)}, u32[]{:S(2)}, u32[]{:S(2)}) collective-permute-start(bf16[8,2,48,384]{3,2,1,0:T(8,128)(2,1)S(1)} %get-tuple-element.37.even_ref), channel_id=1, source_target_pairs={{32,0},{64,32},{96,64},{128,96},{160,128},{192,160},{224,192},{256... | collective-permute-start | bytes 1769480 | tf_op jit(solution)/shard_map/ppermute | solution.py:191
  157.4 12.6 %collective-permute-start.2 = (bf16[8,2,48,384]{3,2,1,0:T(8,128)(2,1)S(1)}, bf16[8,2,48,384]{3,2,1,0:T(8,128)(2,1)S(1)}, u32[]{:S(2)}, u32[]{:S(2)}) collective-permute-start(bf16[8,2,48,384]{3,2,1,0:T(8,128)(2,1)S(1)} %get-tuple-element.36.odd_ref), channel_id=1, source_target_pairs={{992,0},{0,32},{32,64},{64,96},{96,128},{128,160},{160,192},{192,2... | collective-permute-start | bytes 1769480 | tf_op jit(solution)/shard_map/ppermute | solution.py:191
  167.9 2.1 copy-start.6
  170.0 0.8 copy-start.7
  170.8 5.1 %copy-start.9 = (f32[128]{0:T(128)S(1)}, f32[128]{0:T(128)}, u32[]{:S(2)}) copy-start(f32[128]{0:T(128)} %reduce_sum.99) | copy-start | bytes 1540
  175.1 16.4 %copy-start.10 = (f32[2,512]{1,0:T(2,128)S(1)}, f32[2,512]{1,0:T(2,128)}, u32[]{:S(2)}) copy-start(f32[2,512]{1,0:T(2,128)} %get-tuple-element.13) | copy-start | bytes 12292
  175.1 41.3 %copy-start.1 = (bf16[512,384]{0,1:T(8,128)(2,1)S(1)}, bf16[512,384]{0,1:T(8,128)(2,1)}, u32[]{:S(2)}) copy-start(bf16[512,384]{0,1:T(8,128)(2,1)} %copy-done) | copy-start | bytes 1179652
  175.1 41.3 %copy-start.5 = (f32[384,512]{1,0:T(8,128)S(1)}, f32[384,512]{1,0:T(8,128)}, u32[]{:S(2)}) copy-start(f32[384,512]{1,0:T(8,128)} %get-tuple-element.12) | copy-start | bytes 2359300
  175.9 3.1 %collective-permute-start.4 = (f32[4,128]{1,0:T(4,128)S(1)}, f32[4,128]{1,0:T(4,128)S(1)}, u32[]{:S(2)}, u32[]{:S(2)}) collective-permute-start(f32[4,128]{1,0:T(4,128)S(1)} %maximum_bitcast_fusion), channel_id=1, source_target_pairs={{0,16},{16,0},{1,17},{17,1},{2,18},{18,2},{3,19},{19,3},{4,20},{20... | collective-permute-start | bytes 6152 | tf_op jit(solution)/shard_map/ppermute | solution.py:186
  180.7 57.7 %all-to-all-start.2 = ((bf16[8,56,384]{2,1,0:T(8,128)(2,1)}), bf16[8,56,384]{2,1,0:T(8,128)(2,1)S(1)}, u32[]{:S(2)}, u32[]{:S(2)}) async-start(bf16[8,56,384]{2,1,0:T(8,128)(2,1)} %pad_maximum_fusion), calls=%async_computation.2 | async-start | bytes 688128 | tf_op jit(solution)/shard_map/all_to_all | solution.py:165
Sparse Core Ops, SparseCore 0:
  59.1 94.5 all-gather.5

commit v4 on v0

--- a/solution.py
+++ b/solution.py
@@ -13,7 +13,7 @@
 FAR, NEAR = 8, 4
 COLS = 48
 MP = ("x", "y")
-DP = ("far", "near", "core")
+DP = ("far", "high", "low", "core")
 
 
 def qk_kernel(
@@ -89,7 +89,7 @@
 
 
 def input_kernel(
-    near_ref, own_ref, other_ref, query_own_ref, query_other_ref, x_ref, stat_ref, gain_ref,
+    at_ref, own_ref, other_ref, query_own_ref, query_other_ref, x_ref, stat_ref, gain_ref,
     slope_ref, sums_ref, gains_ref, grad_ref,
 ):
     step = pl.program_id(0)
@@ -122,20 +122,20 @@
         gains_ref[...] = jnp.sum(jnp.transpose(lanes), axis=0, keepdims=True)
 
 
-def input_backward(near, own, other, query_own, query_other, x, stat, gain):
+def input_backward(at, own, other, query_own, query_other, x, stat, gain):
     rows, tokens = x.shape
     span = own.shape[0] // NEAR
-    whole = lambda i, near: (0, 0)
+    whole = lambda i, at: (0, 0)
     return pl.pallas_call(
         input_kernel,
         grid_spec=pltpu.PrefetchScalarGridSpec(
             num_scalar_prefetch=1,
             grid=(NEAR,),
             in_specs=[
-                pl.BlockSpec((span, rows), lambda i, near: (i, 0)),
-                pl.BlockSpec((span, rows), lambda i, near: (i, 0)),
-                pl.BlockSpec((1, span, tokens), lambda i, near: ((near[0] + i) % NEAR, 0, 0)),
-                pl.BlockSpec((1, span, tokens), lambda i, near: ((near[0] + i) % NEAR, 0, 0)),
+                pl.BlockSpec((span, rows), lambda i, at: (i, 0)),
+                pl.BlockSpec((span, rows), lambda i, at: (i, 0)),
+                pl.BlockSpec((1, span, tokens), lambda i, at: (2 * (i % 2) + (at[0] + i // 2) % 2, 0, 0)),
+                pl.BlockSpec((1, span, tokens), lambda i, at: (2 * (i % 2) + (at[0] + i // 2) % 2, 0, 0)),
                 pl.BlockSpec((rows, tokens), whole),
                 pl.BlockSpec((2, tokens), whole),
                 pl.BlockSpec((rows, 1), whole),
@@ -156,7 +156,7 @@
         cost_estimate=pl.CostEstimate(
             flops=2_400_000_000, bytes_accessed=7_000_000, transcendentals=0
         ),
-    )(near, own, other, query_own, query_other, x, stat, gain)
+    )(at, own, other, query_own, query_other, x, stat, gain)
 
 
 def exchange(x, axes):
@@ -166,6 +166,12 @@
 def shared_by(x, axes):
     copies = jnp.broadcast_to(x[None], (lax.axis_size(axes), *x.shape))
     return exchange(copies, axes)
+
+
+def thirds(x):
+    high = lax.reduce_precision(x, 8, 7)
+    middle = lax.reduce_precision(x - high, 8, 7)
+    return jnp.stack([high, middle, x - high - middle]).astype(jnp.bfloat16)
 
 
 def summed(x, axes):
@@ -180,29 +186,28 @@
 
 def from_chip(x, distance):
     chips = FAR * NEAR
-    return lax.ppermute(x, ("far", "near"), [((i + distance) % chips, i) for i in range(chips)])
+    return lax.ppermute(x, ("far", "high", "low"), [((i + distance) % chips, i) for i in range(chips)])
 
 
 def shards(block_input, prenorm_gain, weight, query, grad_normed, qk_gain):
     tokens, rows = block_input.shape
-    core = lax.axis_index("core").astype(jnp.int32).reshape(1)
-    near = lax.axis_index("near").astype(jnp.int32).reshape(1)
-
-    own = shared_by(weight.T, "far")
-    after = from_chip(own, 1)
-    before = from_chip(own, -1)
-    half = FAR // 2
-    across = [from_chip(own[:half], 2), from_chip(own[half:], -2)]
-    own = jnp.concatenate([own, after, *across, before]).reshape(-1, rows)
+    core = lax.axis_index("core").astype(jnp.int32)
+    parity = lax.axis_index("low").astype(jnp.int32).reshape(1)
+
+    own = lax.all_gather(weight.T, ("far", "high"), axis=0).reshape(FAR, 2, COLS, rows)
+    even, odd = own[:, 0], own[:, 1]
+    theirs_even = from_chip(even, 1)
+    theirs_odd = from_chip(odd, -1)
+    own = jnp.concatenate([even, odd, theirs_even, theirs_odd]).reshape(-1, rows)
     other = swapped(own)
 
     x_turned = block_input.T
     x = x_turned.astype(jnp.float32)
     sums = jnp.concatenate([jnp.sum(x, axis=0), jnp.sum(x * x, axis=0)]).reshape(8, 128)
-    sums = summed(sums, MP)
-    sums = sums.reshape(2, tokens)
-
-    query_own, query_other, qk_partial = qk_backward(core, query, grad_normed, qk_gain)
+    sums = shared_by(sums, MP)
+    sums = jnp.sum(sums, axis=0).reshape(2, tokens)
+
+    query_own, query_other, qk_partial = qk_backward(core.reshape(1), query, grad_normed, qk_gain)
 
     mean = sums[0:1] / D
     inv = lax.rsqrt(sums[1:2] / D - mean * mean + EPS)
@@ -220,25 +225,30 @@
     from_core = swapped(part)
     part = weight_part(query_own) + from_core.astype(jnp.float32)
     part = part.astype(jnp.bfloat16).reshape(NEAR, FAR, COLS, rows)
-    part = exchange(part, "near")
+    part = exchange(part, ("high", "low"))
     part = jnp.sum(part.astype(jnp.float32), axis=0).astype(jnp.bfloat16)
-    part = exchange(part, "far")
-    grad_weight = jnp.sum(part.astype(jnp.float32), axis=0).T
 
     slope, slopes, gains = input_backward(
-        near, own, other, query_own.reshape(NEAR, -1, tokens),
+        parity, own, other, query_own.reshape(NEAR, -1, tokens),
         query_other.reshape(NEAR, -1, tokens), x_turned, jnp.concatenate([mean, inv]), gain,
     )
     slopes = summed(slopes.reshape(8, 128), MP).reshape(2, tokens) / D
     input_gradient = (inv * (slope - slopes[0:1] - xhat * slopes[1:2])).astype(jnp.bfloat16).T
 
-    gains = jnp.concatenate([gains[0], jnp.sum(qk_partial, axis=0)]).reshape(4, 128)
-    gains = summed(gains + swapped(gains), ("near", "far")).reshape(-1)
+    gains = jnp.concatenate([gains[0], jnp.sum(qk_partial, axis=0)])
+    gains = gains + swapped(gains.reshape(4, 128)).reshape(-1)
+    rest = jnp.pad(thirds(gains).reshape(-1, rows), ((0, 4), (0, 0)))
+    part = jnp.concatenate([part, jnp.broadcast_to(rest[None], (FAR, *rest.shape))], axis=1)
+    part = exchange(part, "far")
+    part = jnp.sum(part.astype(jnp.float32), axis=0)
+    grad_weight = part[:COLS].T
+    gains = jnp.sum(part[COLS : COLS + 4].reshape(3, 4, 128), axis=0)
+    gains = jnp.sum(lax.all_gather(gains, ("high", "low"), axis=0), axis=0).reshape(-1)
     return (input_gradient, grad_weight, gains[:rows], gains[rows:])
 
 
 def solution(mesh):
-    finer = Mesh(mesh.devices.reshape(FAR, NEAR, 2, 4, 4), (*DP, *MP))
+    finer = Mesh(mesh.devices.reshape(FAR, 2, 2, 2, 4, 4), (*DP, *MP))
     in_specs = (P(DP, MP), P(MP), P(MP, DP), P(DP, None), P(DP, None), P())
     out_specs = (P(DP, MP), P(MP, DP), P(MP), P())
 

time: 248 us -> 217 us (0.88)
  the two profiles are of different devices: /device:TPU:8 before, /device:TPU:2 now
where the time goes in v4:
time: 217 us; the launch traced here: 216 us
  blocking collectives  108 us (50%)
  starting transfers between devices  45.2 us (21%)
  waiting for transfers between devices  25.6 us (12%)
  Pallas kernels  22.8 us (11%)
  local copies, waits for them, and re-layouts  5.42 us (2%)
  matrix products  4.75 us (2%)
  other arithmetic  3.7 us (2%)
    all_gather x1, blocking collectives, shards(): lax.all_gather(weight.T, ('far', 'high'), axis=0)  64.7 us
    all_to_all x3, starting transfers between devices, exchange(): return lax.all_to_all(x, axes, 0, 0, tiled=True)  33.2 us
    all_gather x2, blocking collectives, summed(): x = jnp.sum(lax.all_gather(x, axis, axis=0), axis=0)  24.3 us
    all_gather x1, blocking collectives, shards(): lax.all_gather(gains, ('high', 'low'), axis=0)  18.9 us
    pallas_call x1, Pallas kernels, qk_backward(): pl.pallas_call(qk_kernel, grid=(tokens // block,), in_specs=[pl.BlockSpec...  16.5 us
    all_to_all x3, waiting for transfers between devices, exchange(): return lax.all_to_all(x, axes, 0, 0, tiled=True)  13.3 us
    ppermute x2, waiting for transfers between devices, from_chip(): lax.ppermute(x, ('far', 'high', 'low'), [((i + distance) % chips, i) for...  6.94 us
    pallas_call x1, Pallas kernels, input_backward(): pl.pallas_call(input_kernel, grid_spec=pltpu.PrefetchScalarGridSpec(num_s...  6.29 us
  transfers between devices with their start and end apart: 8, of which 6 were waited for; matrix products, arithmetic and copies ran while one was open for 2% of the time, Pallas kernels for 11%

profile of v4, /device:TPU:2, one launch (start us, length us, event | category | flops | bytes accessed | tf_op | source)
XLA Modules:
  0.0 216.1 jit_solution(9469129921931673850)
XLA Ops:
  0.6 1.2 copy.24
  2.6 16.5 %all-to-all-start = ((f32[16,8,128]{2,1,0:T(8,128)}), f32[16,8,128]{2,1,0:T(8,128)S(1)}, u32[]{:S(2)}, u32[]{:S(2)}) async-start(f32[16,8,128]{2,1,0:T(8,128)} %broadcast_in_dim.6), calls=%async_computation | async-start | bytes 131072 | tf_op jit(solution)/shard_map/all_to_all | solution.py:163
  19.1 16.5 %shard_map.93 = (bf16[4,8,48,512]{3,2,1,0:T(8,128)(2,1)}, bf16[4,8,48,512]{3,2,1,0:T(8,128)(2,1)}, f32[8,128]{1,0:T(8,128)}) custom-call(s32[1]{0:T(128)} %bitcast.11.core_ref, bf16[512,3072]{1,0:T(8,128)(2,1)} %query_ref.1, bf16[512,3072]{1,0:T(8,128)(2,1)} %grad_ref.1, f32[1,128]{1,0:T(1,128)} %bitcast.78), custom_call_target="tpu_custom_call" | custom-call | flops 60000000 | bytes 9500000 | tf_op jit(solution)/shard_map/pallas_call | solution.py:64
  35.6 2.6 %convolution_convert_fusion = bf16[1536,384]{1,0:T(8,128)(2,1)S(1)} fusion(bf16[1536,512]{1,0:T(8,128)(2,1)} %bitcast.81, f32[384]{0:T(512)S(1)} %copy-done.7, f32[512]{0:T(512)S(1)} %get-tuple-element.40, f32[512]{0:T(512)S(1)} %fusion.16, bf16[512,384]{0,1:T(8,128)(2,1)S(1)} %copy.24), kind=kOutput, calls=%fused_computation | convolution fusion | flops 605552640 | bytes 3151360 | tf_op jit(solution)/shard_map/dot_general | solution.py:219
  38.2 1.9 collective-permute-start.3
  40.1 2.8 %collective-permute-done.3 = bf16[1536,384]{1,0:T(8,128)(2,1)S(1)} collective-permute-done((bf16[1536,384]{1,0:T(8,128)(2,1)S(1)}, bf16[1536,384]{1,0:T(8,128)(2,1)S(1)}, u32[]{:S(2)}, u32[]{:S(2)}) %collective-permute-start.3) | collective-permute-done | bytes 1179680 | tf_op jit(solution)/shard_map/ppermute | solution.py:184
  43.0 2.1 add_convert_fusion
  45.1 3.7 %all-to-all-start.1 = ((bf16[4,8,48,384]{3,2,1,0:T(8,128)(2,1)}), bf16[4,8,48,384]{3,2,1,0:T(8,128)(2,1)S(1)}, u32[]{:S(2)}, u32[]{:S(2)}) async-start(bf16[4,8,48,384]{3,2,1,0:T(8,128)(2,1)} %bitcast.23), calls=%async_computation.1 | async-start | bytes 2359296 | tf_op jit(solution)/shard_map/all_to_all | solution.py:163
  48.8 64.7 %all-gather = bf16[768,384]{1,0:T(8,128)(2,1)S(1)} all-gather(bf16[48,384]{1,0:T(8,128)(2,1)S(1)} %bitcast.69), channel_id=2, replica_groups=mesh['far'=8,'high'=2,'low'=2,'core'=2,'x'=4,'y'=4] {'far','high'}, dimensions={0}, use_global_device_ids=true | all-gather | bytes 626688 | tf_op jit(solution)/shard_map/all_gather | solution.py:197
  113.6 3.2 %collective-permute-start = (bf16[8,48,384]{2,1,0:T(8,128)(2,1)S(1)}, bf16[8,48,384]{2,1,0:T(8,128)(2,1)S(1)}, u32[]{:S(2)}, u32[]{:S(2)}) collective-permute-start(bf16[8,48,384]{2,1,0:T(8,128)(2,1)S(1)} %get-tuple-element.36), channel_id=1, source_target_pairs={{32,0},{64,32},{96,64},{128,96},{160,128},{192,160},{224,192},{256... | collective-permute-start | bytes 884744 | tf_op jit(solution)/shard_map/ppermute | solution.py:189
  116.8 2.9 %collective-permute-start.1 = (bf16[8,48,384]{2,1,0:T(8,128)(2,1)S(1)}, bf16[8,48,384]{2,1,0:T(8,128)(2,1)S(1)}, u32[]{:S(2)}, u32[]{:S(2)}) collective-permute-start(bf16[8,48,384]{2,1,0:T(8,128)(2,1)S(1)} %get-tuple-element.37), channel_id=1, source_target_pairs={{992,0},{0,32},{32,64},{64,96},{96,128},{128,160},{160,192},{192,2... | collective-permute-start | bytes 884744 | tf_op jit(solution)/shard_map/ppermute | solution.py:189
  119.7 2.7 %collective-permute-done = bf16[8,48,384]{2,1,0:T(8,128)(2,1)S(1)} collective-permute-done((bf16[8,48,384]{2,1,0:T(8,128)(2,1)S(1)}, bf16[8,48,384]{2,1,0:T(8,128)(2,1)S(1)}, u32[]{:S(2)}, u32[]{:S(2)}) %collective-permute-start) | collective-permute-done | bytes 294944 | tf_op jit(solution)/shard_map/ppermute | solution.py:189
  122.5 4.2 %collective-permute-done.1 = bf16[8,48,384]{2,1,0:T(8,128)(2,1)S(1)} collective-permute-done((bf16[8,48,384]{2,1,0:T(8,128)(2,1)S(1)}, bf16[8,48,384]{2,1,0:T(8,128)(2,1)S(1)}, u32[]{:S(2)}, u32[]{:S(2)}) %collective-permute-start.1) | collective-permute-done | bytes 294944 | tf_op jit(solution)/shard_map/ppermute | solution.py:189
  126.8 1.9 collective-permute-start.2
  130.2 1.5 collective-permute-done.2.other_ref
  131.7 6.3 %shard_map.94 = (f32[384,512]{1,0:T(8,128)}, f32[2,512]{1,0:T(2,128)}, f32[1,384]{1,0:T(1,128)}) custom-call(s32[1]{0:T(128)} %bitcast.5.at_ref, bf16[1536,384]{1,0:T(8,128)(2,1)} %bitcast.68, bf16[1536,384]{1,0:T(8,128)(2,1)} %collective-permute-done.2.other_ref, bf16[4,384,512]{2,1,0:T(8,128)(2,1)} %bitcast.79, bf16[4,384,512]{2,1,0:T(8,128)(2,1)} %bitcast.82, ...), custom_call_target="tpu_custom_call" | custom-call | flops 2400000000 | bytes 7000000 | tf_op jit(solution)/shard_map/pallas_call | solution.py:129
  138.7 2.0 collective-permute-start.4
  140.8 1.0 collective-permute-done.4
  143.6 13.1 %all-to-all-start.2 = ((bf16[8,56,384]{2,1,0:T(8,128)(2,1)}), bf16[8,56,384]{2,1,0:T(8,128)(2,1)S(1)}, u32[]{:S(2)}, u32[]{:S(2)}) async-start(bf16[8,56,384]{2,1,0:T(8,128)(2,1)} %pad_maximum_fusion.1), calls=%async_computation.2 | async-start | bytes 688128 | tf_op jit(solution)/shard_map/all_to_all | solution.py:163
  156.7 12.0 %all_gather.23 = f32[4,8,128]{2,1,0:T(8,128)S(1)} all-gather(f32[1,8,128]{2,1,0:T(8,128)S(1)} %all_gather_reshape.3), channel_id=1, replica_groups=mesh['far'=8,'high'=2,'low'=2,'core'=2,'x'=4,'y'=4] {'x'}, dimensions={0}, use_global_device_ids=true | all-gather | bytes 20480 | tf_op jit(solution)/shard_map/all_gather | solution.py:179
  168.7 12.3 %all-gather.1 = f32[32,128]{1,0:T(8,128)S(1)} all-gather(f32[8,128]{1,0:T(8,128)S(1)} %reduce_sum.96), channel_id=3, replica_groups=mesh['far'=8,'high'=2,'low'=2,'core'=2,'x'=4,'y'=4] {'y'}, dimensions={0}, use_global_device_ids=true | all-gather | bytes 20480 | tf_op jit(solution)/shard_map/all_gather | solution.py:179
  181.2 0.9 copy.28
  182.2 13.3 %all-to-all-done.2 = bf16[8,56,384]{2,1,0:T(8,128)(2,1)S(1)} async-done(((bf16[8,56,384]{2,1,0:T(8,128)(2,1)}), bf16[8,56,384]{2,1,0:T(8,128)(2,1)S(1)}, u32[]{:S(2)}, u32[]{:S(2)}) %all-to-all-start.2) | async-done | bytes 344096 | tf_op jit(solution)/shard_map/all_to_all | solution.py:163
  196.2 18.9 %all-gather.3 = f32[4,4,128]{2,1,0:T(4,128)S(1)} all-gather(f32[1,4,128]{2,1,0:T(4,128)S(1)} %bitcast.75), channel_id=4, replica_groups=mesh['far'=8,'high'=2,'low'=2,'core'=2,'x'=4,'y'=4] {'high','low'}, dimensions={0}, use_global_device_ids=true | all-gather | bytes 10240 | tf_op jit(solution)/shard_map/all_gather | solution.py:246
  (56 shorter events, 7.0 us)
Async XLA Ops:
  1.8 41.2 %copy-start = (bf16[512,384]{0,1:T(8,128)(2,1)}, bf16[512,384]{0,1:T(8,128)(2,1)S(1)}, u32[]{:S(2)}) copy-start(bf16[512,384]{0,1:T(8,128)(2,1)S(1)} %copy.24) | copy-start | bytes 1179652
  2.6 32.9 %all-to-all-start = ((f32[16,8,128]{2,1,0:T(8,128)}), f32[16,8,128]{2,1,0:T(8,128)S(1)}, u32[]{:S(2)}, u32[]{:S(2)}) async-start(f32[16,8,128]{2,1,0:T(8,128)} %broadcast_in_dim.6), calls=%async_computation | async-start | bytes 131072 | tf_op jit(solution)/shard_map/all_to_all | solution.py:163
  19.1 16.5 %copy-start.7 = (f32[384]{0:T(512)S(1)}, f32[384]{0:T(512)}, u32[]{:S(2)}) copy-start(f32[384]{0:T(512)} %param.7) | copy-start | bytes 4612
  35.6 7.4 %copy-start.8 = (bf16[4,8,48,512]{3,2,1,0:T(8,128)(2,1)S(1)}, bf16[4,8,48,512]{3,2,1,0:T(8,128)(2,1)}, u32[]{:S(2)}) copy-start(bf16[4,8,48,512]{3,2,1,0:T(8,128)(2,1)} %get-tuple-element.10) | copy-start | bytes 4718596
  38.2 4.7 %collective-permute-start.3 = (bf16[1536,384]{1,0:T(8,128)(2,1)S(1)}, bf16[1536,384]{1,0:T(8,128)(2,1)S(1)}, u32[]{:S(2)}, u32[]{:S(2)}) collective-permute-start(bf16[1536,384]{1,0:T(8,128)(2,1)S(1)} %convolution_convert_fusion), channel_id=1, source_target_pairs={{0,16},{16,0},{1,17},{17,1},{2,18},{18,2},{3,19},{19,3},{4,20},{20... | collective-permute-start | bytes 3538952 | tf_op jit(solution)/shard_map/ppermute | solution.py:184
  45.1 3.7 %copy-start.4 = (bf16[384,48]{0,1:T(8,128)(2,1)S(1)}, bf16[384,48]{0,1:T(8,128)(2,1)}, u32[]{:S(2)}) copy-start(bf16[384,48]{0,1:T(8,128)(2,1)} %param.8) | copy-start | bytes 110596
  45.1 97.5 %all-to-all-start.1 = ((bf16[4,8,48,384]{3,2,1,0:T(8,128)(2,1)}), bf16[4,8,48,384]{3,2,1,0:T(8,128)(2,1)S(1)}, u32[]{:S(2)}, u32[]{:S(2)}) async-start(bf16[4,8,48,384]{3,2,1,0:T(8,128)(2,1)} %bitcast.23), calls=%async_computation.1 | async-start | bytes 2359296 | tf_op jit(solution)/shard_map/all_to_all | solution.py:163
  113.6 8.9 %collective-permute-start = (bf16[8,48,384]{2,1,0:T(8,128)(2,1)S(1)}, bf16[8,48,384]{2,1,0:T(8,128)(2,1)S(1)}, u32[]{:S(2)}, u32[]{:S(2)}) collective-permute-start(bf16[8,48,384]{2,1,0:T(8,128)(2,1)S(1)} %get-tuple-element.36), channel_id=1, source_target_pairs={{32,0},{64,32},{96,64},{128,96},{160,128},{192,160},{224,192},{256... | collective-permute-start | bytes 884744 | tf_op jit(solution)/shard_map/ppermute | solution.py:189
  116.8 12.8 %copy-start.5 = (f32[8,128]{1,0:T(8,128)S(1)}, f32[8,128]{1,0:T(8,128)}, u32[]{:S(2)}) copy-start(f32[8,128]{1,0:T(8,128)} %get-tuple-element.15) | copy-start | bytes 12292
  116.8 9.8 %collective-permute-start.1 = (bf16[8,48,384]{2,1,0:T(8,128)(2,1)S(1)}, bf16[8,48,384]{2,1,0:T(8,128)(2,1)S(1)}, u32[]{:S(2)}, u32[]{:S(2)}) collective-permute-start(bf16[8,48,384]{2,1,0:T(8,128)(2,1)S(1)} %get-tuple-element.37), channel_id=1, source_target_pairs={{992,0},{0,32},{32,64},{64,96},{96,128},{128,160},{160,192},{192,2... | collective-permute-start | bytes 884744 | tf_op jit(solution)/shard_map/ppermute | solution.py:189
  126.8 4.9 %copy-start.2 = (bf16[32,48,384]{2,1,0:T(8,128)(2,1)}, bf16[32,48,384]{2,1,0:T(8,128)(2,1)S(1)}, u32[]{:S(2)}) copy-start(bf16[32,48,384]{2,1,0:T(8,128)(2,1)S(1)} %pad_maximum_fusion) | copy-start | bytes 3538948
  126.8 4.9 %collective-permute-start.2 = (bf16[1536,384]{1,0:T(8,128)(2,1)S(1)}, bf16[1536,384]{1,0:T(8,128)(2,1)}, u32[]{:S(2)}, u32[]{:S(2)}) collective-permute-start(bf16[1536,384]{1,0:T(8,128)(2,1)S(1)} %bitcast.67), channel_id=1, source_target_pairs={{0,16},{16,0},{1,17},{17,1},{2,18},{18,2},{3,19},{19,3},{4,20},{20... | collective-permute-start | bytes 3538952 | tf_op jit(solution)/shard_map/ppermute | solution.py:184
  138.7 3.1 %collective-permute-start.4 = (f32[4,128]{1,0:T(4,128)S(1)}, f32[4,128]{1,0:T(4,128)S(1)}, u32[]{:S(2)}, u32[]{:S(2)}) collective-permute-start(f32[4,128]{1,0:T(4,128)S(1)} %maximum_bitcast_fusion), channel_id=1, source_target_pairs={{0,16},{16,0},{1,17},{17,1},{2,18},{18,2},{3,19},{19,3},{4,20},{20... | collective-permute-start | bytes 6152 | tf_op jit(solution)/shard_map/ppermute | solution.py:184
  142.5 14.1 %copy-start.6 = (f32[2,512]{1,0:T(2,128)S(1)}, f32[2,512]{1,0:T(2,128)}, u32[]{:S(2)}) copy-start(f32[2,512]{1,0:T(2,128)} %get-tuple-element.13) | copy-start | bytes 12292
  142.5 38.5 %copy-start.1 = (bf16[512,384]{0,1:T(8,128)(2,1)S(1)}, bf16[512,384]{0,1:T(8,128)(2,1)}, u32[]{:S(2)}) copy-start(bf16[512,384]{0,1:T(8,128)(2,1)} %copy-done) | copy-start | bytes 1179652
  142.6 38.5 %copy-start.3 = (f32[384,512]{1,0:T(8,128)S(1)}, f32[384,512]{1,0:T(8,128)}, u32[]{:S(2)}) copy-start(f32[384,512]{1,0:T(8,128)} %get-tuple-element.12) | copy-start | bytes 2359300
  143.6 51.8 %all-to-all-start.2 = ((bf16[8,56,384]{2,1,0:T(8,128)(2,1)}), bf16[8,56,384]{2,1,0:T(8,128)(2,1)S(1)}, u32[]{:S(2)}, u32[]{:S(2)}) async-start(bf16[8,56,384]{2,1,0:T(8,128)(2,1)} %pad_maximum_fusion.1), calls=%async_computation.2 | async-start | bytes 688128 | tf_op jit(solution)/shard_map/all_to_all | solution.py:163

commit v5 on v4

--- a/solution.py
+++ b/solution.py
@@ -236,14 +236,15 @@
     input_gradient = (inv * (slope - slopes[0:1] - xhat * slopes[1:2])).astype(jnp.bfloat16).T
 
     gains = jnp.concatenate([gains[0], jnp.sum(qk_partial, axis=0)])
-    gains = gains + swapped(gains.reshape(4, 128)).reshape(-1)
+    gains = gains.reshape(4, 128)
+    gains = gains + swapped(gains)
+    gains = jnp.sum(lax.all_gather(gains, ("high", "low"), axis=0), axis=0).reshape(-1)
     rest = jnp.pad(thirds(gains).reshape(-1, rows), ((0, 4), (0, 0)))
     part = jnp.concatenate([part, jnp.broadcast_to(rest[None], (FAR, *rest.shape))], axis=1)
     part = exchange(part, "far")
     part = jnp.sum(part.astype(jnp.float32), axis=0)
     grad_weight = part[:COLS].T
-    gains = jnp.sum(part[COLS : COLS + 4].reshape(3, 4, 128), axis=0)
-    gains = jnp.sum(lax.all_gather(gains, ("high", "low"), axis=0), axis=0).reshape(-1)
+    gains = jnp.sum(part[COLS : COLS + 4].reshape(3, -1), axis=0)
     return (input_gradient, grad_weight, gains[:rows], gains[rows:])
 
 

time: 217 us -> 213 us (0.982)
  the two profiles are of different devices: /device:TPU:2 before, /device:TPU:68 now
where the time goes in v5:
time: 213 us
  blocking collectives  98.2 us (46%)
  starting transfers between devices  44.7 us (21%)
  waiting for transfers between devices  33.5 us (16%)
  Pallas kernels  22.8 us (11%)
  local copies, waits for them, and re-layouts  4.9 us (2%)
  matrix products  4.75 us (2%)
  other arithmetic  3.03 us (1%)
    all_gather x1, blocking collectives, shards(): lax.all_gather(weight.T, ('far', 'high'), axis=0)  63.4 us
    all_to_all x3, starting transfers between devices, exchange(): return lax.all_to_all(x, axes, 0, 0, tiled=True)  32.8 us
    all_gather x2, blocking collectives, summed(): x = jnp.sum(lax.all_gather(x, axis, axis=0), axis=0)  23.1 us
    all_to_all x3, waiting for transfers between devices, exchange(): return lax.all_to_all(x, axes, 0, 0, tiled=True)  21.4 us
    pallas_call x1, Pallas kernels, qk_backward(): pl.pallas_call(qk_kernel, grid=(tokens // block,), in_specs=[pl.BlockSpec...  16.5 us
    all_gather x1, blocking collectives, shards(): lax.all_gather(gains, ('high', 'low'), axis=0)  11.7 us
    ppermute x2, waiting for transfers between devices, from_chip(): lax.ppermute(x, ('far', 'high', 'low'), [((i + distance) % chips, i) for...  6.69 us
    pallas_call x1, Pallas kernels, input_backward(): pl.pallas_call(input_kernel, grid_spec=pltpu.PrefetchScalarGridSpec(num_s...  6.29 us
  transfers between devices with their start and end apart: 8, of which 6 were waited for; matrix products, arithmetic and copies ran while one was open for 2% of the time, Pallas kernels for 11%

profile of v5, /device:TPU:68, one launch (start us, length us, event | category | flops | bytes accessed | tf_op | source)
XLA Modules:
  0.0 212.6 jit_solution(6507366612701993026)
XLA Ops:
  0.6 1.2 copy.24
  2.6 7.5 %all-to-all-start = ((f32[16,8,128]{2,1,0:T(8,128)}), f32[16,8,128]{2,1,0:T(8,128)S(1)}, u32[]{:S(2)}, u32[]{:S(2)}) async-start(f32[16,8,128]{2,1,0:T(8,128)} %broadcast_in_dim.6), calls=%async_computation | async-start | bytes 131072 | tf_op jit(solution)/shard_map/all_to_all | solution.py:163
  10.1 16.5 %shard_map.93 = (bf16[4,8,48,512]{3,2,1,0:T(8,128)(2,1)}, bf16[4,8,48,512]{3,2,1,0:T(8,128)(2,1)}, f32[8,128]{1,0:T(8,128)}) custom-call(s32[1]{0:T(128)} %bitcast.11.core_ref, bf16[512,3072]{1,0:T(8,128)(2,1)} %query_ref.1, bf16[512,3072]{1,0:T(8,128)(2,1)} %grad_ref.1, f32[1,128]{1,0:T(1,128)} %bitcast.76), custom_call_target="tpu_custom_call" | custom-call | flops 60000000 | bytes 9500000 | tf_op jit(solution)/shard_map/pallas_call | solution.py:64
  26.6 2.6 %convolution_convert_fusion = bf16[1536,384]{1,0:T(8,128)(2,1)S(1)} fusion(bf16[1536,512]{1,0:T(8,128)(2,1)} %bitcast.79, f32[384]{0:T(512)S(1)} %copy-done.7, f32[512]{0:T(512)S(1)} %get-tuple-element.38, f32[512]{0:T(512)S(1)} %fusion.16, bf16[512,384]{0,1:T(8,128)(2,1)S(1)} %copy.24), kind=kOutput, calls=%fused_computation | convolution fusion | flops 605552640 | bytes 3151360 | tf_op jit(solution)/shard_map/dot_general | solution.py:219
  29.2 1.9 collective-permute-start.3
  31.1 2.8 %collective-permute-done.3 = bf16[1536,384]{1,0:T(8,128)(2,1)S(1)} collective-permute-done((bf16[1536,384]{1,0:T(8,128)(2,1)S(1)}, bf16[1536,384]{1,0:T(8,128)(2,1)S(1)}, u32[]{:S(2)}, u32[]{:S(2)}) %collective-permute-start.3) | collective-permute-done | bytes 1179680 | tf_op jit(solution)/shard_map/ppermute | solution.py:184
  34.0 2.1 %add_convert_fusion = bf16[1536,384]{1,0:T(8,128)(2,1)} fusion(bf16[1536,384]{1,0:T(8,128)(2,1)S(1)} %collective-permute-done.3, bf16[1536,512]{1,0:T(8,128)(2,1)S(1)} %bitcast.78, f32[384]{0:T(512)S(1)} %copy-done.7, f32[512]{0:T(512)S(1)} %get-tuple-element.38, f32[512]{0:T(512)S(1)} %fusion.16, bf16[512,384]{0,1:T(8,128)(2,1)S(1)} %copy.24), kind=kOutput, calls=%fused_computation.1 | convolution fusion | flops 606732288 | bytes 4331008 | tf_op jit(solution)/shard_map/dot_general | solution.py:219
  36.1 12.3 %all-to-all-start.1 = ((bf16[4,8,48,384]{3,2,1,0:T(8,128)(2,1)}), bf16[4,8,48,384]{3,2,1,0:T(8,128)(2,1)S(1)}, u32[]{:S(2)}, u32[]{:S(2)}) async-start(bf16[4,8,48,384]{3,2,1,0:T(8,128)(2,1)} %bitcast.23), calls=%async_computation.1 | async-start | bytes 2359296 | tf_op jit(solution)/shard_map/all_to_all | solution.py:163
  48.4 63.4 %all-gather = bf16[768,384]{1,0:T(8,128)(2,1)S(1)} all-gather(bf16[48,384]{1,0:T(8,128)(2,1)S(1)} %bitcast.68), channel_id=2, replica_groups=mesh['far'=8,'high'=2,'low'=2,'core'=2,'x'=4,'y'=4] {'far','high'}, dimensions={0}, use_global_device_ids=true | all-gather | bytes 626688 | tf_op jit(solution)/shard_map/all_gather | solution.py:197
  111.9 4.1 %collective-permute-start = (bf16[8,48,384]{2,1,0:T(8,128)(2,1)S(1)}, bf16[8,48,384]{2,1,0:T(8,128)(2,1)S(1)}, u32[]{:S(2)}, u32[]{:S(2)}) collective-permute-start(bf16[8,48,384]{2,1,0:T(8,128)(2,1)S(1)} %get-tuple-element.34), channel_id=1, source_target_pairs={{32,0},{64,32},{96,64},{128,96},{160,128},{192,160},{224,192},{256... | collective-permute-start | bytes 884744 | tf_op jit(solution)/shard_map/ppermute | solution.py:189
  115.9 1.9 collective-permute-start.1
  117.9 2.6 %collective-permute-done = bf16[8,48,384]{2,1,0:T(8,128)(2,1)S(1)} collective-permute-done((bf16[8,48,384]{2,1,0:T(8,128)(2,1)S(1)}, bf16[8,48,384]{2,1,0:T(8,128)(2,1)S(1)}, u32[]{:S(2)}, u32[]{:S(2)}) %collective-permute-start) | collective-permute-done | bytes 294944 | tf_op jit(solution)/shard_map/ppermute | solution.py:189
  120.5 4.1 %collective-permute-done.1 = bf16[8,48,384]{2,1,0:T(8,128)(2,1)S(1)} collective-permute-done((bf16[8,48,384]{2,1,0:T(8,128)(2,1)S(1)}, bf16[8,48,384]{2,1,0:T(8,128)(2,1)S(1)}, u32[]{:S(2)}, u32[]{:S(2)}) %collective-permute-start.1) | collective-permute-done | bytes 294944 | tf_op jit(solution)/shard_map/ppermute | solution.py:189
  124.8 1.9 collective-permute-start.2
  128.1 1.5 collective-permute-done.2.other_ref
  129.6 6.3 %shard_map.94 = (f32[384,512]{1,0:T(8,128)}, f32[2,512]{1,0:T(2,128)}, f32[1,384]{1,0:T(1,128)}) custom-call(s32[1]{0:T(128)} %bitcast.5.at_ref, bf16[1536,384]{1,0:T(8,128)(2,1)} %bitcast.67, bf16[1536,384]{1,0:T(8,128)(2,1)} %collective-permute-done.2.other_ref, bf16[4,384,512]{2,1,0:T(8,128)(2,1)} %bitcast.77, bf16[4,384,512]{2,1,0:T(8,128)(2,1)} %bitcast.80, ...), custom_call_target="tpu_custom_call" | custom-call | flops 2400000000 | bytes 7000000 | tf_op jit(solution)/shard_map/pallas_call | solution.py:129
  136.6 2.0 collective-permute-start.4
  138.7 1.0 collective-permute-done.4
  139.7 11.7 %all-gather.3 = f32[4,4,128]{2,1,0:T(4,128)S(1)} all-gather(f32[1,4,128]{2,1,0:T(4,128)S(1)} %add_bitcast_fusion), channel_id=4, replica_groups=mesh['far'=8,'high'=2,'low'=2,'core'=2,'x'=4,'y'=4] {'high','low'}, dimensions={0}, use_global_device_ids=true | all-gather | bytes 10240 | tf_op jit(solution)/shard_map/all_gather | solution.py:241
  152.5 13.1 %all-to-all-start.2 = ((bf16[8,56,384]{2,1,0:T(8,128)(2,1)}), bf16[8,56,384]{2,1,0:T(8,128)(2,1)S(1)}, u32[]{:S(2)}, u32[]{:S(2)}) async-start(bf16[8,56,384]{2,1,0:T(8,128)(2,1)} %pad_maximum_fusion.1), calls=%async_computation.2 | async-start | bytes 688128 | tf_op jit(solution)/shard_map/all_to_all | solution.py:163
  165.6 10.8 %all_gather.23 = f32[4,8,128]{2,1,0:T(8,128)S(1)} all-gather(f32[1,8,128]{2,1,0:T(8,128)S(1)} %all_gather_reshape.3), channel_id=1, replica_groups=mesh['far'=8,'high'=2,'low'=2,'core'=2,'x'=4,'y'=4] {'x'}, dimensions={0}, use_global_device_ids=true | all-gather | bytes 20480 | tf_op jit(solution)/shard_map/all_gather | solution.py:179
  176.4 12.3 %all-gather.1 = f32[32,128]{1,0:T(8,128)S(1)} all-gather(f32[8,128]{1,0:T(8,128)S(1)} %reduce_sum.96), channel_id=3, replica_groups=mesh['far'=8,'high'=2,'low'=2,'core'=2,'x'=4,'y'=4] {'y'}, dimensions={0}, use_global_device_ids=true | all-gather | bytes 20480 | tf_op jit(solution)/shard_map/all_gather | solution.py:179
  188.9 0.9 copy.28
  189.9 21.4 %all-to-all-done.2 = bf16[8,56,384]{2,1,0:T(8,128)(2,1)S(1)} async-done(((bf16[8,56,384]{2,1,0:T(8,128)(2,1)}), bf16[8,56,384]{2,1,0:T(8,128)(2,1)S(1)}, u32[]{:S(2)}, u32[]{:S(2)}) %all-to-all-start.2) | async-done | bytes 344096 | tf_op jit(solution)/shard_map/all_to_all | solution.py:163
  (57 shorter events, 5.9 us)
Async XLA Ops:
  1.8 32.1 %copy-start = (bf16[512,384]{0,1:T(8,128)(2,1)}, bf16[512,384]{0,1:T(8,128)(2,1)S(1)}, u32[]{:S(2)}) copy-start(bf16[512,384]{0,1:T(8,128)(2,1)S(1)} %copy.24) | copy-start | bytes 1179652
  2.6 23.9 %all-to-all-start = ((f32[16,8,128]{2,1,0:T(8,128)}), f32[16,8,128]{2,1,0:T(8,128)S(1)}, u32[]{:S(2)}, u32[]{:S(2)}) async-start(f32[16,8,128]{2,1,0:T(8,128)} %broadcast_in_dim.6), calls=%async_computation | async-start | bytes 131072 | tf_op jit(solution)/shard_map/all_to_all | solution.py:163
  10.1 16.5 %copy-start.7 = (f32[384]{0:T(512)S(1)}, f32[384]{0:T(512)}, u32[]{:S(2)}) copy-start(f32[384]{0:T(512)} %param.7) | copy-start | bytes 4612
  26.6 7.4 %copy-start.9 = (bf16[4,8,48,512]{3,2,1,0:T(8,128)(2,1)S(1)}, bf16[4,8,48,512]{3,2,1,0:T(8,128)(2,1)}, u32[]{:S(2)}) copy-start(bf16[4,8,48,512]{3,2,1,0:T(8,128)(2,1)} %get-tuple-element.10) | copy-start | bytes 4718596
  29.2 4.7 %collective-permute-start.3 = (bf16[1536,384]{1,0:T(8,128)(2,1)S(1)}, bf16[1536,384]{1,0:T(8,128)(2,1)S(1)}, u32[]{:S(2)}, u32[]{:S(2)}) collective-permute-start(bf16[1536,384]{1,0:T(8,128)(2,1)S(1)} %convolution_convert_fusion), channel_id=1, source_target_pairs={{0,16},{16,0},{1,17},{17,1},{2,18},{18,2},{3,19},{19,3},{4,20},{20... | collective-permute-start | bytes 3538952 | tf_op jit(solution)/shard_map/ppermute | solution.py:184
  36.1 12.3 %copy-start.4 = (bf16[384,48]{0,1:T(8,128)(2,1)S(1)}, bf16[384,48]{0,1:T(8,128)(2,1)}, u32[]{:S(2)}) copy-start(bf16[384,48]{0,1:T(8,128)(2,1)} %param.8) | copy-start | bytes 110596
  36.1 115.4 %all-to-all-start.1 = ((bf16[4,8,48,384]{3,2,1,0:T(8,128)(2,1)}), bf16[4,8,48,384]{3,2,1,0:T(8,128)(2,1)S(1)}, u32[]{:S(2)}, u32[]{:S(2)}) async-start(bf16[4,8,48,384]{3,2,1,0:T(8,128)(2,1)} %bitcast.23), calls=%async_computation.1 | async-start | bytes 2359296 | tf_op jit(solution)/shard_map/all_to_all | solution.py:163
  111.9 8.6 %collective-permute-start = (bf16[8,48,384]{2,1,0:T(8,128)(2,1)S(1)}, bf16[8,48,384]{2,1,0:T(8,128)(2,1)S(1)}, u32[]{:S(2)}, u32[]{:S(2)}) collective-permute-start(bf16[8,48,384]{2,1,0:T(8,128)(2,1)S(1)} %get-tuple-element.34), channel_id=1, source_target_pairs={{32,0},{64,32},{96,64},{128,96},{160,128},{192,160},{224,192},{256... | collective-permute-start | bytes 884744 | tf_op jit(solution)/shard_map/ppermute | solution.py:189
  115.9 11.6 %copy-start.5 = (f32[8,128]{1,0:T(8,128)S(1)}, f32[8,128]{1,0:T(8,128)}, u32[]{:S(2)}) copy-start(f32[8,128]{1,0:T(8,128)} %get-tuple-element.15) | copy-start | bytes 12292
  115.9 8.6 %collective-permute-start.1 = (bf16[8,48,384]{2,1,0:T(8,128)(2,1)S(1)}, bf16[8,48,384]{2,1,0:T(8,128)(2,1)S(1)}, u32[]{:S(2)}, u32[]{:S(2)}) collective-permute-start(bf16[8,48,384]{2,1,0:T(8,128)(2,1)S(1)} %get-tuple-element.35), channel_id=1, source_target_pairs={{992,0},{0,32},{32,64},{64,96},{96,128},{128,160},{160,192},{192,2... | collective-permute-start | bytes 884744 | tf_op jit(solution)/shard_map/ppermute | solution.py:189
  124.8 4.9 %copy-start.2 = (bf16[32,48,384]{2,1,0:T(8,128)(2,1)}, bf16[32,48,384]{2,1,0:T(8,128)(2,1)S(1)}, u32[]{:S(2)}) copy-start(bf16[32,48,384]{2,1,0:T(8,128)(2,1)S(1)} %pad_maximum_fusion) | copy-start | bytes 3538948
  124.8 4.9 %collective-permute-start.2 = (bf16[1536,384]{1,0:T(8,128)(2,1)S(1)}, bf16[1536,384]{1,0:T(8,128)(2,1)}, u32[]{:S(2)}, u32[]{:S(2)}) collective-permute-start(bf16[1536,384]{1,0:T(8,128)(2,1)S(1)} %bitcast.66), channel_id=1, source_target_pairs={{0,16},{16,0},{1,17},{17,1},{2,18},{18,2},{3,19},{19,3},{4,20},{20... | collective-permute-start | bytes 3538952 | tf_op jit(solution)/shard_map/ppermute | solution.py:184
  136.6 3.1 %collective-permute-start.4 = (f32[4,128]{1,0:T(4,128)S(1)}, f32[4,128]{1,0:T(4,128)S(1)}, u32[]{:S(2)}, u32[]{:S(2)}) collective-permute-start(f32[4,128]{1,0:T(4,128)S(1)} %maximum_bitcast_fusion), channel_id=1, source_target_pairs={{0,16},{16,0},{1,17},{17,1},{2,18},{18,2},{3,19},{19,3},{4,20},{20... | collective-permute-start | bytes 6152 | tf_op jit(solution)/shard_map/ppermute | solution.py:184
  151.5 14.1 %copy-start.6 = (f32[2,512]{1,0:T(2,128)S(1)}, f32[2,512]{1,0:T(2,128)}, u32[]{:S(2)}) copy-start(f32[2,512]{1,0:T(2,128)} %get-tuple-element.13) | copy-start | bytes 12292
  151.5 37.3 %copy-start.1 = (bf16[512,384]{0,1:T(8,128)(2,1)S(1)}, bf16[512,384]{0,1:T(8,128)(2,1)}, u32[]{:S(2)}) copy-start(bf16[512,384]{0,1:T(8,128)(2,1)} %copy-done) | copy-start | bytes 1179652
  151.5 37.3 %copy-start.3 = (f32[384,512]{1,0:T(8,128)S(1)}, f32[384,512]{1,0:T(8,128)}, u32[]{:S(2)}) copy-start(f32[384,512]{1,0:T(8,128)} %get-tuple-element.12) | copy-start | bytes 2359300
  152.5 58.8 %all-to-all-start.2 = ((bf16[8,56,384]{2,1,0:T(8,128)(2,1)}), bf16[8,56,384]{2,1,0:T(8,128)(2,1)S(1)}, u32[]{:S(2)}, u32[]{:S(2)}) async-start(bf16[8,56,384]{2,1,0:T(8,128)(2,1)} %pad_maximum_fusion.1), calls=%async_computation.2 | async-start | bytes 688128 | tf_op jit(solution)/shard_map/all_to_all | solution.py:163
  212.0 0.6 copy-start.8

commit v6 on v5

--- a/solution.py
+++ b/solution.py
@@ -30,19 +30,22 @@
     def three_heads(group, total):
         for j in range(3):
             cols = pl.ds(pl.multiple_of(group * 384 + j * HEAD, HEAD), HEAD)
-            q = query_ref[:, cols].astype(jnp.float32)
-            upstream = grad_ref[:, cols].astype(jnp.float32)
-            mean = jnp.sum(q, axis=1, keepdims=True) * scale
-            var = jnp.sum(q * q, axis=1, keepdims=True) * scale - mean * mean
-            inv = lax.rsqrt(var + EPS)
-            qhat = (q - mean) * inv
-            dqhat = upstream * gain
-            mean_d = jnp.sum(dqhat, axis=1, keepdims=True) * scale
-            mean_c = jnp.sum(dqhat * qhat, axis=1, keepdims=True) * scale
-            rows_ref[:, j * HEAD : (j + 1) * HEAD] = (
-                inv * (dqhat - mean_d - qhat * mean_c)
-            ).astype(jnp.bfloat16)
-            total = total + jnp.sum((upstream * qhat).reshape(-1, 8, HEAD), axis=0)
+            for r in range(0, query_ref.shape[0], 32):
+                at = pl.ds(r, 32)
+                q = query_ref[at, cols].astype(jnp.float32)
+                upstream = grad_ref[at, cols].astype(jnp.float32)
+                dqhat = upstream * gain
+                mean = jnp.sum(q, axis=1, keepdims=True) * scale
+                mean_d = jnp.sum(dqhat, axis=1, keepdims=True) * scale
+                square = jnp.sum(q * q, axis=1, keepdims=True) * scale
+                cross = jnp.sum(dqhat * q, axis=1, keepdims=True) * scale
+                inv = lax.rsqrt(square - mean * mean + EPS)
+                mean_c = (cross - mean * mean_d) * inv
+                qhat = (q - mean) * inv
+                rows_ref[at, j * HEAD : (j + 1) * HEAD] = (
+                    inv * (dqhat - mean_d - qhat * mean_c)
+                ).astype(jnp.bfloat16)
+                total = total + jnp.sum((upstream * qhat).reshape(-1, 8, HEAD), axis=0)
         turned = jnp.transpose(rows_ref[...])
         for parity, (even_ref, odd_ref) in enumerate(((own_ref, other_ref), (other_ref, own_ref))):
 

time: 213 us -> 211 us (level)
  the two profiles are of different devices: /device:TPU:68 before, /device:TPU:66 now
where the time goes in v6:
time: 211 us; the launch traced here: 210 us
  blocking collectives  99.4 us (47%)
  starting transfers between devices  44.7 us (21%)
  waiting for transfers between devices  32.3 us (15%)
  Pallas kernels  20.3 us (10%)
  local copies, waits for them, and re-layouts  4.9 us (2%)
  matrix products  4.75 us (2%)
  other arithmetic  3.03 us (1%)
    all_gather x1, blocking collectives, shards(): lax.all_gather(weight.T, ('far', 'high'), axis=0)  63.4 us
    all_to_all x3, starting transfers between devices, exchange(): return lax.all_to_all(x, axes, 0, 0, tiled=True)  32.8 us
    all_gather x2, blocking collectives, summed(): x = jnp.sum(lax.all_gather(x, axis, axis=0), axis=0)  24.3 us
    all_to_all x3, waiting for transfers between devices, exchange(): return lax.all_to_all(x, axes, 0, 0, tiled=True)  20.3 us
    pallas_call x1, Pallas kernels, qk_backward(): pl.pallas_call(qk_kernel, grid=(tokens // block,), in_specs=[pl.BlockSpec...  14 us
    all_gather x1, blocking collectives, shards(): lax.all_gather(gains, ('high', 'low'), axis=0)  11.7 us
    ppermute x2, waiting for transfers between devices, from_chip(): lax.ppermute(x, ('far', 'high', 'low'), [((i + distance) % chips, i) for...  6.69 us
    pallas_call x1, Pallas kernels, input_backward(): pl.pallas_call(input_kernel, grid_spec=pltpu.PrefetchScalarGridSpec(num_s...  6.29 us
  transfers between devices with their start and end apart: 8, of which 6 were waited for; matrix products, arithmetic and copies ran while one was open for 2% of the time, Pallas kernels for 10%

profile of v6, /device:TPU:66, one launch (start us, length us, event | category | flops | bytes accessed | tf_op | source)
XLA Modules:
  0.0 210.2 jit_solution(12428623891308923447)
XLA Ops:
  0.6 1.2 copy.24
  2.6 7.5 %all-to-all-start = ((f32[16,8,128]{2,1,0:T(8,128)}), f32[16,8,128]{2,1,0:T(8,128)S(1)}, u32[]{:S(2)}, u32[]{:S(2)}) async-start(f32[16,8,128]{2,1,0:T(8,128)} %broadcast_in_dim.6), calls=%async_computation | async-start | bytes 131072 | tf_op jit(solution)/shard_map/all_to_all | solution.py:166
  10.1 14.0 %shard_map.93 = (bf16[4,8,48,512]{3,2,1,0:T(8,128)(2,1)}, bf16[4,8,48,512]{3,2,1,0:T(8,128)(2,1)}, f32[8,128]{1,0:T(8,128)}) custom-call(s32[1]{0:T(128)} %bitcast.11.core_ref, bf16[512,3072]{1,0:T(8,128)(2,1)} %query_ref.1, bf16[512,3072]{1,0:T(8,128)(2,1)} %grad_ref.1, f32[1,128]{1,0:T(1,128)} %bitcast.76), custom_call_target="tpu_custom_call" | custom-call | flops 60000000 | bytes 9500000 | tf_op jit(solution)/shard_map/pallas_call | solution.py:67
  24.1 2.6 %convolution_convert_fusion = bf16[1536,384]{1,0:T(8,128)(2,1)S(1)} fusion(bf16[1536,512]{1,0:T(8,128)(2,1)} %bitcast.79, f32[384]{0:T(512)S(1)} %copy-done.7, f32[512]{0:T(512)S(1)} %get-tuple-element.38, f32[512]{0:T(512)S(1)} %fusion.16, bf16[512,384]{0,1:T(8,128)(2,1)S(1)} %copy.24), kind=kOutput, calls=%fused_computation | convolution fusion | flops 605552640 | bytes 3151360 | tf_op jit(solution)/shard_map/dot_general | solution.py:222
  26.7 1.9 collective-permute-start.3
  28.7 2.8 %collective-permute-done.3 = bf16[1536,384]{1,0:T(8,128)(2,1)S(1)} collective-permute-done((bf16[1536,384]{1,0:T(8,128)(2,1)S(1)}, bf16[1536,384]{1,0:T(8,128)(2,1)S(1)}, u32[]{:S(2)}, u32[]{:S(2)}) %collective-permute-start.3) | collective-permute-done | bytes 1179680 | tf_op jit(solution)/shard_map/ppermute | solution.py:187
  31.5 2.1 %add_convert_fusion = bf16[1536,384]{1,0:T(8,128)(2,1)} fusion(bf16[1536,384]{1,0:T(8,128)(2,1)S(1)} %collective-permute-done.3, bf16[1536,512]{1,0:T(8,128)(2,1)S(1)} %bitcast.78, f32[384]{0:T(512)S(1)} %copy-done.7, f32[512]{0:T(512)S(1)} %get-tuple-element.38, f32[512]{0:T(512)S(1)} %fusion.16, bf16[512,384]{0,1:T(8,128)(2,1)S(1)} %copy.24), kind=kOutput, calls=%fused_computation.1 | convolution fusion | flops 606732288 | bytes 4331008 | tf_op jit(solution)/shard_map/dot_general | solution.py:222
  33.6 12.3 %all-to-all-start.1 = ((bf16[4,8,48,384]{3,2,1,0:T(8,128)(2,1)}), bf16[4,8,48,384]{3,2,1,0:T(8,128)(2,1)S(1)}, u32[]{:S(2)}, u32[]{:S(2)}) async-start(bf16[4,8,48,384]{3,2,1,0:T(8,128)(2,1)} %bitcast.23), calls=%async_computation.1 | async-start | bytes 2359296 | tf_op jit(solution)/shard_map/all_to_all | solution.py:166
  45.9 63.4 %all-gather = bf16[768,384]{1,0:T(8,128)(2,1)S(1)} all-gather(bf16[48,384]{1,0:T(8,128)(2,1)S(1)} %bitcast.68), channel_id=2, replica_groups=mesh['far'=8,'high'=2,'low'=2,'core'=2,'x'=4,'y'=4] {'far','high'}, dimensions={0}, use_global_device_ids=true | all-gather | bytes 626688 | tf_op jit(solution)/shard_map/all_gather | solution.py:200
  109.4 4.1 %collective-permute-start = (bf16[8,48,384]{2,1,0:T(8,128)(2,1)S(1)}, bf16[8,48,384]{2,1,0:T(8,128)(2,1)S(1)}, u32[]{:S(2)}, u32[]{:S(2)}) collective-permute-start(bf16[8,48,384]{2,1,0:T(8,128)(2,1)S(1)} %get-tuple-element.34), channel_id=1, source_target_pairs={{32,0},{64,32},{96,64},{128,96},{160,128},{192,160},{224,192},{256... | collective-permute-start | bytes 884744 | tf_op jit(solution)/shard_map/ppermute | solution.py:192
  113.5 1.9 collective-permute-start.1
  115.4 2.6 %collective-permute-done = bf16[8,48,384]{2,1,0:T(8,128)(2,1)S(1)} collective-permute-done((bf16[8,48,384]{2,1,0:T(8,128)(2,1)S(1)}, bf16[8,48,384]{2,1,0:T(8,128)(2,1)S(1)}, u32[]{:S(2)}, u32[]{:S(2)}) %collective-permute-start) | collective-permute-done | bytes 294944 | tf_op jit(solution)/shard_map/ppermute | solution.py:192
  118.0 4.1 %collective-permute-done.1 = bf16[8,48,384]{2,1,0:T(8,128)(2,1)S(1)} collective-permute-done((bf16[8,48,384]{2,1,0:T(8,128)(2,1)S(1)}, bf16[8,48,384]{2,1,0:T(8,128)(2,1)S(1)}, u32[]{:S(2)}, u32[]{:S(2)}) %collective-permute-start.1) | collective-permute-done | bytes 294944 | tf_op jit(solution)/shard_map/ppermute | solution.py:192
  122.3 1.9 collective-permute-start.2
  125.7 1.5 collective-permute-done.2.other_ref
  127.2 6.3 %shard_map.94 = (f32[384,512]{1,0:T(8,128)}, f32[2,512]{1,0:T(2,128)}, f32[1,384]{1,0:T(1,128)}) custom-call(s32[1]{0:T(128)} %bitcast.5.at_ref, bf16[1536,384]{1,0:T(8,128)(2,1)} %bitcast.67, bf16[1536,384]{1,0:T(8,128)(2,1)} %collective-permute-done.2.other_ref, bf16[4,384,512]{2,1,0:T(8,128)(2,1)} %bitcast.77, bf16[4,384,512]{2,1,0:T(8,128)(2,1)} %bitcast.80, ...), custom_call_target="tpu_custom_call" | custom-call | flops 2400000000 | bytes 7000000 | tf_op jit(solution)/shard_map/pallas_call | solution.py:132
  134.2 2.0 collective-permute-start.4
  136.2 1.0 collective-permute-done.4
  137.2 11.7 %all-gather.3 = f32[4,4,128]{2,1,0:T(4,128)S(1)} all-gather(f32[1,4,128]{2,1,0:T(4,128)S(1)} %add_bitcast_fusion), channel_id=4, replica_groups=mesh['far'=8,'high'=2,'low'=2,'core'=2,'x'=4,'y'=4] {'high','low'}, dimensions={0}, use_global_device_ids=true | all-gather | bytes 10240 | tf_op jit(solution)/shard_map/all_gather | solution.py:244
  150.0 13.1 %all-to-all-start.2 = ((bf16[8,56,384]{2,1,0:T(8,128)(2,1)}), bf16[8,56,384]{2,1,0:T(8,128)(2,1)S(1)}, u32[]{:S(2)}, u32[]{:S(2)}) async-start(bf16[8,56,384]{2,1,0:T(8,128)(2,1)} %pad_maximum_fusion.1), calls=%async_computation.2 | async-start | bytes 688128 | tf_op jit(solution)/shard_map/all_to_all | solution.py:166
  163.1 12.0 %all_gather.23 = f32[4,8,128]{2,1,0:T(8,128)S(1)} all-gather(f32[1,8,128]{2,1,0:T(8,128)S(1)} %all_gather_reshape.3), channel_id=1, replica_groups=mesh['far'=8,'high'=2,'low'=2,'core'=2,'x'=4,'y'=4] {'x'}, dimensions={0}, use_global_device_ids=true | all-gather | bytes 20480 | tf_op jit(solution)/shard_map/all_gather | solution.py:182
  175.2 12.3 %all-gather.1 = f32[32,128]{1,0:T(8,128)S(1)} all-gather(f32[8,128]{1,0:T(8,128)S(1)} %reduce_sum.96), channel_id=3, replica_groups=mesh['far'=8,'high'=2,'low'=2,'core'=2,'x'=4,'y'=4] {'y'}, dimensions={0}, use_global_device_ids=true | all-gather | bytes 20480 | tf_op jit(solution)/shard_map/all_gather | solution.py:182
  187.7 0.9 copy.28
  188.6 20.3 %all-to-all-done.2 = bf16[8,56,384]{2,1,0:T(8,128)(2,1)S(1)} async-done(((bf16[8,56,384]{2,1,0:T(8,128)(2,1)}), bf16[8,56,384]{2,1,0:T(8,128)(2,1)S(1)}, u32[]{:S(2)}, u32[]{:S(2)}) %all-to-all-start.2) | async-done | bytes 344096 | tf_op jit(solution)/shard_map/all_to_all | solution.py:166
  (57 shorter events, 5.9 us)
Async XLA Ops:
  1.8 29.7 %copy-start = (bf16[512,384]{0,1:T(8,128)(2,1)}, bf16[512,384]{0,1:T(8,128)(2,1)S(1)}, u32[]{:S(2)}) copy-start(bf16[512,384]{0,1:T(8,128)(2,1)S(1)} %copy.24) | copy-start | bytes 1179652
  2.6 21.5 %all-to-all-start = ((f32[16,8,128]{2,1,0:T(8,128)}), f32[16,8,128]{2,1,0:T(8,128)S(1)}, u32[]{:S(2)}, u32[]{:S(2)}) async-start(f32[16,8,128]{2,1,0:T(8,128)} %broadcast_in_dim.6), calls=%async_computation | async-start | bytes 131072 | tf_op jit(solution)/shard_map/all_to_all | solution.py:166
  10.1 14.0 %copy-start.7 = (f32[384]{0:T(512)S(1)}, f32[384]{0:T(512)}, u32[]{:S(2)}) copy-start(f32[384]{0:T(512)} %param.7) | copy-start | bytes 4612
  24.1 7.4 %copy-start.9 = (bf16[4,8,48,512]{3,2,1,0:T(8,128)(2,1)S(1)}, bf16[4,8,48,512]{3,2,1,0:T(8,128)(2,1)}, u32[]{:S(2)}) copy-start(bf16[4,8,48,512]{3,2,1,0:T(8,128)(2,1)} %get-tuple-element.10) | copy-start | bytes 4718596
  26.7 4.7 %collective-permute-start.3 = (bf16[1536,384]{1,0:T(8,128)(2,1)S(1)}, bf16[1536,384]{1,0:T(8,128)(2,1)S(1)}, u32[]{:S(2)}, u32[]{:S(2)}) collective-permute-start(bf16[1536,384]{1,0:T(8,128)(2,1)S(1)} %convolution_convert_fusion), channel_id=1, source_target_pairs={{0,16},{16,0},{1,17},{17,1},{2,18},{18,2},{3,19},{19,3},{4,20},{20... | collective-permute-start | bytes 3538952 | tf_op jit(solution)/shard_map/ppermute | solution.py:187
  33.6 12.3 %copy-start.4 = (bf16[384,48]{0,1:T(8,128)(2,1)S(1)}, bf16[384,48]{0,1:T(8,128)(2,1)}, u32[]{:S(2)}) copy-start(bf16[384,48]{0,1:T(8,128)(2,1)} %param.8) | copy-start | bytes 110596
  33.6 115.4 %all-to-all-start.1 = ((bf16[4,8,48,384]{3,2,1,0:T(8,128)(2,1)}), bf16[4,8,48,384]{3,2,1,0:T(8,128)(2,1)S(1)}, u32[]{:S(2)}, u32[]{:S(2)}) async-start(bf16[4,8,48,384]{3,2,1,0:T(8,128)(2,1)} %bitcast.23), calls=%async_computation.1 | async-start | bytes 2359296 | tf_op jit(solution)/shard_map/all_to_all | solution.py:166
  109.4 8.6 %collective-permute-start = (bf16[8,48,384]{2,1,0:T(8,128)(2,1)S(1)}, bf16[8,48,384]{2,1,0:T(8,128)(2,1)S(1)}, u32[]{:S(2)}, u32[]{:S(2)}) collective-permute-start(bf16[8,48,384]{2,1,0:T(8,128)(2,1)S(1)} %get-tuple-element.34), channel_id=1, source_target_pairs={{32,0},{64,32},{96,64},{128,96},{160,128},{192,160},{224,192},{256... | collective-permute-start | bytes 884744 | tf_op jit(solution)/shard_map/ppermute | solution.py:192
  113.5 11.6 %copy-start.5 = (f32[8,128]{1,0:T(8,128)S(1)}, f32[8,128]{1,0:T(8,128)}, u32[]{:S(2)}) copy-start(f32[8,128]{1,0:T(8,128)} %get-tuple-element.15) | copy-start | bytes 12292
  113.5 8.6 %collective-permute-start.1 = (bf16[8,48,384]{2,1,0:T(8,128)(2,1)S(1)}, bf16[8,48,384]{2,1,0:T(8,128)(2,1)S(1)}, u32[]{:S(2)}, u32[]{:S(2)}) collective-permute-start(bf16[8,48,384]{2,1,0:T(8,128)(2,1)S(1)} %get-tuple-element.35), channel_id=1, source_target_pairs={{992,0},{0,32},{32,64},{64,96},{96,128},{128,160},{160,192},{192,2... | collective-permute-start | bytes 884744 | tf_op jit(solution)/shard_map/ppermute | solution.py:192
  122.3 4.9 %copy-start.2 = (bf16[32,48,384]{2,1,0:T(8,128)(2,1)}, bf16[32,48,384]{2,1,0:T(8,128)(2,1)S(1)}, u32[]{:S(2)}) copy-start(bf16[32,48,384]{2,1,0:T(8,128)(2,1)S(1)} %pad_maximum_fusion) | copy-start | bytes 3538948
  122.3 4.9 %collective-permute-start.2 = (bf16[1536,384]{1,0:T(8,128)(2,1)S(1)}, bf16[1536,384]{1,0:T(8,128)(2,1)}, u32[]{:S(2)}, u32[]{:S(2)}) collective-permute-start(bf16[1536,384]{1,0:T(8,128)(2,1)S(1)} %bitcast.66), channel_id=1, source_target_pairs={{0,16},{16,0},{1,17},{17,1},{2,18},{18,2},{3,19},{19,3},{4,20},{20... | collective-permute-start | bytes 3538952 | tf_op jit(solution)/shard_map/ppermute | solution.py:187
  134.2 3.1 %collective-permute-start.4 = (f32[4,128]{1,0:T(4,128)S(1)}, f32[4,128]{1,0:T(4,128)S(1)}, u32[]{:S(2)}, u32[]{:S(2)}) collective-permute-start(f32[4,128]{1,0:T(4,128)S(1)} %maximum_bitcast_fusion), channel_id=1, source_target_pairs={{0,16},{16,0},{1,17},{17,1},{2,18},{18,2},{3,19},{19,3},{4,20},{20... | collective-permute-start | bytes 6152 | tf_op jit(solution)/shard_map/ppermute | solution.py:187
  149.0 14.1 %copy-start.6 = (f32[2,512]{1,0:T(2,128)S(1)}, f32[2,512]{1,0:T(2,128)}, u32[]{:S(2)}) copy-start(f32[2,512]{1,0:T(2,128)} %get-tuple-element.13) | copy-start | bytes 12292
  149.0 38.5 %copy-start.1 = (bf16[512,384]{0,1:T(8,128)(2,1)S(1)}, bf16[512,384]{0,1:T(8,128)(2,1)}, u32[]{:S(2)}) copy-start(bf16[512,384]{0,1:T(8,128)(2,1)} %copy-done) | copy-start | bytes 1179652
  149.0 38.5 %copy-start.3 = (f32[384,512]{1,0:T(8,128)S(1)}, f32[384,512]{1,0:T(8,128)}, u32[]{:S(2)}) copy-start(f32[384,512]{1,0:T(8,128)} %get-tuple-element.12) | copy-start | bytes 2359300
  150.0 58.8 %all-to-all-start.2 = ((bf16[8,56,384]{2,1,0:T(8,128)(2,1)}), bf16[8,56,384]{2,1,0:T(8,128)(2,1)S(1)}, u32[]{:S(2)}, u32[]{:S(2)}) async-start(bf16[8,56,384]{2,1,0:T(8,128)(2,1)} %pad_maximum_fusion.1), calls=%async_computation.2 | async-start | bytes 688128 | tf_op jit(solution)/shard_map/all_to_all | solution.py:166
  209.6 0.6 copy-start.8
